TPU v7x, 32 devices: a whole 2x2x4 slice. The times are simulated.
32 devices in a mesh: genes: 32 (over z, y, x, core).
Axes of the slice: x: 2, y: 2, z: 4, core: 2. Of those that a mesh axis runs over, the one named last changes fastest.
Arguments:
- expression: bfloat16 [32768, 1024], P('genes'), may hold values from -10 to 20
- labels: int32 [32768], P('genes'), may hold values from 0 to 399
Outputs:
- membership: float32 [32768, 400], P('genes')
- eigengenes: bfloat16 [400, 1024], replicated
All inputs are finite; a program needn't handle non-finite values.
Results may differ from a plain program's by a relative error of at most 0.0012.
The roundings to bfloat16 on the way count: a program that leaves them out, or rounds other values in their place, can miss the bound.
Values may be sent and summed in bfloat16 or wider, within the bound.
No kernel may reach another device: no remote copies, remote signals or barrier semaphores. Data moves between devices by JAX's collectives and lax.ppermute only.
A program may use at most 64 MiB of HBM per device.

v0:
```python
import jax
import jax.numpy as jnp
from jax import lax
from jax.sharding import PartitionSpec as P

SAMPLES = 1024
MODULES = 400
ITERS = 2


epsilon = 1e-05
sharpness = 30.0


def standardize(expression):
    values = expression.astype(jnp.float32)
    centre = jnp.mean(values, axis=1, keepdims=True)
    shifted = values - centre
    spread = jnp.mean(shifted * shifted, axis=1, keepdims=True)
    return (shifted * lax.rsqrt(spread + epsilon)).astype(jnp.bfloat16)


def shards(expression, labels):
    standard = standardize(expression)
    module_ids = jnp.arange(MODULES, dtype=jnp.int32)
    weights = (labels[:, None] == module_ids[None, :]).astype(jnp.bfloat16)
    shares = None
    eigengenes = None
    for iteration in range(ITERS):
        partial_value = lax.dot_general(
            weights, standard, (((0,), (0,)), ((), ())), preferred_element_type=jnp.float32
        )
        module_sums = lax.psum(partial_value, "genes")
        scale = lax.rsqrt(jnp.mean(module_sums * module_sums, axis=1, keepdims=True) + epsilon)
        eigengenes = (module_sums * scale).astype(jnp.bfloat16)
        correlation = (
            lax.dot_general(
                standard, eigengenes, (((1,), (1,)), ((), ())), preferred_element_type=jnp.float32
            )
            / SAMPLES
        )
        raised = jnp.exp(sharpness * correlation)
        shares = raised / jnp.sum(raised, axis=1, keepdims=True)
        weights = shares.astype(jnp.bfloat16)
    return (MODULES * shares, eigengenes)


def solution(mesh):
    placed = (P("genes", None), P("genes"))
    return jax.shard_map(
        shards, mesh=mesh, in_specs=placed, out_specs=(P("genes", None), P()), check_vma=False
    )
```

profile of v0, /device:TPU:0, one launch (start us, length us, event | category | flops | bytes accessed | tf_op | source)
XLA Modules:
  0.0 299.7 jit_solution(1048506449199865023)
XLA Ops:
  7.2 0.0 copy-start
  7.2 0.0 all-reduce.3.cloned.1.call-start
  7.2 2.1 convert_reduce_fusion
  9.3 0.1 copy-done
  9.4 0.7 fusion.2
  10.1 0.0 copy-start.5
  10.1 0.5 fusion.3
  10.7 0.0 copy-start.2
  10.7 1.3 copy-done.2
  12.0 0.0 copy-done.5
  12.0 2.4 fusion.4
  14.4 0.0 copy-start.3
  14.4 0.0 all-reduce.3.cloned.1.call-update
  14.4 0.0 all-reduce.5.cloned.1.call-start
  14.5 135.1 %all-reduce.3.cloned.1.call-done = f32[400,1024]{1,0:T(8,128)} async-done(((f32[400,1024]{1,0:T(8,128)}), f32[400,1024]{1,0:T(8,128)}) %all-reduce.3.cloned.1.call-update) | async-done | bytes 1638416 | tf_op jit(solution)/shard_map/psum | solution.py:33
  149.6 1.6 multiply_reduce_fusion.1
  151.2 0.0 copy-done.3
  151.2 2.5 fusion.9
  153.7 2.2 fusion.6
  155.9 0.0 all-reduce.5.cloned.1.call-update
  155.9 132.3 %all-reduce.5.cloned.1.call-done = f32[400,1024]{1,0:T(8,128)} async-done(((f32[400,1024]{1,0:T(8,128)}), f32[400,1024]{1,0:T(8,128)}) %all-reduce.5.cloned.1.call-update) | async-done | bytes 1638416 | tf_op jit(solution)/shard_map/psum | solution.py:33
  288.3 0.0 copy-start.1
  288.3 1.7 multiply_reduce_fusion
  290.0 0.2 copy-done.1
  290.2 0.1 multiply_convert_fusion
  290.4 0.0 copy-start.4
  290.4 1.1 fusion.10
  291.5 0.0 copy-done.4
  291.5 1.4 divide_multiply_fusion
  (4 shorter events, 0.0 us)
Async XLA Ops:
  7.2 2.2 copy-start
  7.2 142.4 %all-reduce.3.cloned.1.call-start = ((), (), s32[]{:S(2)}) async-start(), calls=%async_computation | async-start | bytes 3276800 | tf_op jit(solution)/shard_map/psum | solution.py:33
  10.1 1.9 copy-start.5
  10.7 1.4 copy-start.2
  14.4 136.8 %copy-start.3 = (bf16[1024,1024]{1,0:T(8,128)(2,1)S(1)}, bf16[1024,1024]{1,0:T(8,128)(2,1)}, u32[]{:S(2)}) copy-start(bf16[1024,1024]{1,0:T(8,128)(2,1)} %copy-done.2) | copy-start | bytes 6291460
  14.4 273.8 %all-reduce.5.cloned.1.call-start = ((), (), s32[]{:S(2)}) async-start(), calls=%async_computation.1 | async-start | bytes 3276800 | tf_op jit(solution)/shard_map/psum | solution.py:33
  288.3 1.9 copy-start.1
  290.4 1.1 copy-start.4
Sparse Core Ops, SparseCore 0:
  14.6 134.9 all-reduce.2
  156.1 132.1 all-reduce.4
where the time goes:
time: 300 us
  waiting for transfers between devices  267 us (89%)
  between operations  14.1 us (5%)
  other arithmetic  8.28 us (3%)
  matrix products  8.17 us (3%)
    psum x2, waiting for transfers between devices, shards(): module_sums = lax.psum(partial_value, 'genes')  267 us
  transfers between devices with their start and end apart: 2, of which 2 were waited for; matrix products, arithmetic and copies ran while one was open for 0% of the time, Pallas kernels for 0%

commit v1 on v0

v1 whole, which is shorter than its diff:
```python
import math

import jax
import jax.numpy as jnp
from jax import lax
from jax.sharding import PartitionSpec as P

MODULES = 400
ITERS = 2


epsilon = 1e-05
sharpness = 30.0

AXIS = "genes"
BLOCKS = 8
ROW_TILE = 8
HALF_MAX = 60000.0


def standardize(expression):
    values = expression.astype(jnp.float32)
    centre = jnp.mean(values, axis=1, keepdims=True)
    shifted = values - centre
    spread = jnp.mean(shifted * shifted, axis=1, keepdims=True)
    return (shifted * lax.rsqrt(spread + epsilon)).astype(jnp.bfloat16)


def swap(value, devices, bit):
    return lax.ppermute(value, AXIS, [(i, i ^ bit) for i in range(devices)])


def power_below(limit):
    return 2.0 ** math.floor(math.log2(limit))


def reduce_block(sums, devices, bound, sent):
    half = sums.shape[0] // 2
    rows = half // 4
    chip = sums[:half] + swap(sums[half:], devices, 1)
    bound = 2.0 * bound
    down = power_below(HALF_MAX / bound)
    others = [
        swap((chip[k * rows:(k + 1) * rows] * down).astype(sent), devices, 2 * k)
        for k in range(1, 4)
    ]
    others = [other.astype(jnp.float32) for other in others]
    total = ((chip[:rows] * down + others[0]) + (others[1] + others[2])) * (1.0 / down)
    bound = 4.0 * bound
    bit = 8
    while bit < devices:
        steps = range(1, min(4, devices // bit))
        down = power_below(HALF_MAX / bound)
        own = (total * down).astype(sent)
        others = [swap(own, devices, bit * k).astype(jnp.float32) for k in steps]
        total = own.astype(jnp.float32) + others[0]
        if len(others) == 3:
            total = total + (others[1] + others[2])
        total = total * (1.0 / down)
        bound = bound * (len(others) + 1)
        bit = bit * (len(others) + 1)
    return total


def gather_blocks(block, devices):
    half = jnp.concatenate([block] + [swap(block, devices, 2 * k) for k in range(1, 4)], axis=0)
    return jnp.concatenate([half, swap(half, devices, 1)], axis=0)


def shards(devices):
    def body(expression, labels):
        genes, samples = expression.shape
        used = -(-MODULES // BLOCKS)
        rows = -(-used // ROW_TILE) * ROW_TILE
        place = lax.axis_index(AXIS)
        mine = (place & 1) * 4 + ((place >> 1) & 3)
        bound = genes * math.sqrt(samples) * 1.02

        standard = standardize(expression)
        column = jnp.arange(BLOCKS * rows, dtype=jnp.int32)
        slot = ((labels // used) ^ mine) * rows + labels % used
        weights = (slot[:, None] == column[None, :]).astype(jnp.bfloat16)
        for iteration in range(ITERS):
            partial_value = lax.dot_general(
                weights, standard, (((0,), (0,)), ((), ())), preferred_element_type=jnp.float32
            )
            total = reduce_block(partial_value, devices, bound, jnp.float16 if iteration == ITERS - 1 else jnp.float32)
            scale = lax.rsqrt(jnp.mean(total * total, axis=1, keepdims=True) + epsilon)
            block = (total * scale).astype(jnp.bfloat16)
            eigengenes = gather_blocks(block, devices)
            last = iteration == ITERS - 1
            if last:
                blocks = eigengenes.reshape(BLOCKS, rows, samples)[:, :used]
                for bit in (4, 2, 1):
                    pairs = blocks.reshape(BLOCKS // (2 * bit), 2, bit, used, samples)
                    blocks = jnp.where((mine & bit) != 0, pairs[:, ::-1], pairs)
                eigengenes = blocks.reshape(BLOCKS * used, samples)[:MODULES]
            correlation = (
                lax.dot_general(
                    standard, eigengenes, (((1,), (1,)), ((), ())), preferred_element_type=jnp.float32
                )
                / samples
            )
            raised = jnp.exp(sharpness * correlation)
            if not last:
                block_of = column // rows
                number = (block_of ^ mine) * used + column % rows
                real = (column % rows < used) & (number < MODULES)
                raised = jnp.where(real[None, :], raised, 0.0)
            shares = raised / jnp.sum(raised, axis=1, keepdims=True)
            weights = shares.astype(jnp.bfloat16)
        return (MODULES * shares, eigengenes)

    return body


def solution(mesh):
    placed = (P(AXIS, None), P(AXIS))
    return jax.shard_map(
        shards(mesh.shape[AXIS]), mesh=mesh, in_specs=placed, out_specs=(P(AXIS, None), P()), check_vma=False
    )
```

time: 300 us -> 104 us (0.35)
  waiting for transfers between devices: 267 us -> 57.6 us
  starting transfers between devices: 0.08 us -> 26.2 us
  between operations: 14.1 us -> 0.89 us
    psum x2 -> x0, waiting for transfers between devices: 267 us -> none  [shards(): module_sums = lax.psum(partial_value, 'genes')]
    ppermute x0 -> x22, waiting for transfers between devices: none -> 57.6 us  [swap(): return lax.ppermute(value, AXIS, [(i, i ^ bit) for i in range(devices)])]
    ppermute x0 -> x22, starting transfers between devices: none -> 26.2 us  [swap(): return lax.ppermute(value, AXIS, [(i, i ^ bit) for i in range(devices)])]
    reduce_sum x2, other arithmetic: 3.36 us -> 0.32 us  [body(): scale = lax.rsqrt(jnp.mean(total * total, axis=1, keepdims=True) + epsilon)]
  transfers between devices with their start and end apart: 2 -> 22, of which waited for: 2 -> 18; matrix products, arithmetic and copies ran while one was open for 0% -> 0% of each run, Pallas kernels for 0% -> 0%
where the time goes in v1:
time: 104 us; the launch traced here: 103 us
  waiting for transfers between devices  57.6 us (55%)
  starting transfers between devices  26.2 us (25%)
  other arithmetic  8.7 us (8%)
  matrix products  7.44 us (7%)
  local copies, waits for them, and re-layouts  2.56 us (2%)
    ppermute x22, waiting for transfers between devices, swap(): return lax.ppermute(value, AXIS, [(i, i ^ bit) for i in range(devices)])  57.6 us
    ppermute x22, starting transfers between devices, swap(): return lax.ppermute(value, AXIS, [(i, i ^ bit) for i in range(devices)])  26.2 us
    dot_general x2, matrix products, body(): lax.dot_general(weights, standard, (((0,), (0,)), ((), ())), preferred_el...  3.95 us
    dot_general x2, matrix products, body(): lax.dot_general(standard, eigengenes, (((1,), (1,)), ((), ())), preferred...  3.49 us
    reduce_sum x1, other arithmetic, standardize(): centre = jnp.mean(values, axis=1, keepdims=True)  2.08 us
  transfers between devices with their start and end apart: 22, of which 18 were waited for; matrix products, arithmetic and copies ran while one was open for 0% of the time, Pallas kernels for 0%

profile of v1, /device:TPU:0, one launch (start us, length us, event | category | flops | bytes accessed | tf_op | source)
XLA Modules:
  0.0 103.4 jit_solution(7278580747598440753)
XLA Ops:
  0.6 2.1 %convert_reduce_fusion = f32[1024]{0:T(1024)S(1)} fusion(bf16[1024,1024]{1,0:T(8,128)(2,1)} %param.2), kind=kLoop, calls=%fused_computation.1 | loop fusion | flops 2096128 | bytes 2101248 | tf_op jit(solution)/shard_map/reduce_sum | solution.py:23
  2.7 0.1 copy-done
  2.9 0.7 fusion.2
  3.6 1.9 %fusion.3 = bf16[1024,1024]{1,0:T(8,128)(2,1)} fusion(bf16[1024,1024]{1,0:T(8,128)(2,1)S(1)} %copy-done, f32[1024]{0:T(1024)S(1)} %add_rsqrt_fusion, f32[1024]{0:T(1024)S(1)} %broadcast_multiply_fusion), kind=kLoop, calls=%fused_computation.5 | loop fusion | flops 4194304 | bytes 4202496 | tf_op jit(solution)/shard_map/convert_element_type | solution.py:26
  5.5 2.8 %fusion.4 = f32[448,1024]{1,0:T(8,128)S(1)} fusion(bf16[1024,1024]{1,0:T(8,128)(2,1)} %fusion.3, s32[1024]{0:T(1024)S(1)} %fusion.20), kind=kOutput, calls=%fused_computation.7 | convolution fusion | flops 939982848 | bytes 3936256 | tf_op jit(solution)/shard_map/dot_general | solution.py:84
  8.3 0.1 slice.53
  8.4 0.6 collective-permute-start
  8.9 2.1 %collective-permute-done = f32[224,1024]{1,0:T(8,128)S(1)} collective-permute-done((f32[224,1024]{1,0:T(8,128)S(1)}, f32[224,1024]{1,0:T(8,128)S(1)}, u32[]{:S(2)}, u32[]{:S(2)}) %collective-permute-start) | collective-permute-done | bytes 917536 | tf_op jit(solution)/shard_map/ppermute | solution.py:30
  11.0 0.1 slice_add_fusion.1
  11.2 0.1 slice_multiply_fusion.4
  11.3 2.9 %collective-permute-start.1 = (f32[56,1024]{1,0:T(8,128)S(1)}, f32[56,1024]{1,0:T(8,128)S(1)}, u32[]{:S(2)}, u32[]{:S(2)}) collective-permute-start(f32[56,1024]{1,0:T(8,128)S(1)} %get-tuple-element.13), channel_id=1, source_target_pairs={{0,2},{1,3},{2,0},{3,1},{4,6},{5,7},{6,4},{7,5},{8,10},{9,11},{10,... | collective-permute-start | bytes 688136 | tf_op jit(solution)/shard_map/ppermute | solution.py:30
  14.2 1.5 %collective-permute-start.2 = (f32[56,1024]{1,0:T(8,128)S(1)}, f32[56,1024]{1,0:T(8,128)S(1)}, u32[]{:S(2)}, u32[]{:S(2)}) collective-permute-start(f32[56,1024]{1,0:T(8,128)S(1)} %get-tuple-element.12), channel_id=1, source_target_pairs={{0,4},{1,5},{2,6},{3,7},{4,0},{5,1},{6,2},{7,3},{8,12},{9,13},{10,... | collective-permute-start | bytes 688136 | tf_op jit(solution)/shard_map/ppermute | solution.py:30
  15.7 4.9 %collective-permute-done.1 = f32[56,1024]{1,0:T(8,128)S(1)} collective-permute-done((f32[56,1024]{1,0:T(8,128)S(1)}, f32[56,1024]{1,0:T(8,128)S(1)}, u32[]{:S(2)}, u32[]{:S(2)}) %collective-permute-start.1) | collective-permute-done | bytes 229408 | tf_op jit(solution)/shard_map/ppermute | solution.py:30
  20.6 5.8 %collective-permute-done.2 = f32[56,1024]{1,0:T(8,128)S(1)} collective-permute-done((f32[56,1024]{1,0:T(8,128)S(1)}, f32[56,1024]{1,0:T(8,128)S(1)}, u32[]{:S(2)}, u32[]{:S(2)}) %collective-permute-start.2) | collective-permute-done | bytes 229408 | tf_op jit(solution)/shard_map/ppermute | solution.py:30
  26.5 1.6 %collective-permute-start.4 = (f32[56,1024]{1,0:T(8,128)S(1)}, f32[56,1024]{1,0:T(8,128)S(1)}, u32[]{:S(2)}, u32[]{:S(2)}) collective-permute-start(f32[56,1024]{1,0:T(8,128)S(1)} %fusion.17), channel_id=1, source_target_pairs={{0,8},{1,9},{2,10},{3,11},{4,12},{5,13},{6,14},{7,15},{8,0},{9,1},... | collective-permute-start | bytes 688136 | tf_op jit(solution)/shard_map/ppermute | solution.py:30
  28.2 2.6 %collective-permute-start.5 = (f32[56,1024]{1,0:T(8,128)S(1)}, f32[56,1024]{1,0:T(8,128)S(1)}, u32[]{:S(2)}, u32[]{:S(2)}) collective-permute-start(f32[56,1024]{1,0:T(8,128)S(1)} %fusion.17), channel_id=1, source_target_pairs={{0,16},{1,17},{2,18},{3,19},{4,20},{5,21},{6,22},{7,23},{8,24},{9,... | collective-permute-start | bytes 688136 | tf_op jit(solution)/shard_map/ppermute | solution.py:30
  30.8 0.2 collective-permute-start.6
  31.0 5.9 %collective-permute-done.4 = f32[56,1024]{1,0:T(8,128)S(1)} collective-permute-done((f32[56,1024]{1,0:T(8,128)S(1)}, f32[56,1024]{1,0:T(8,128)S(1)}, u32[]{:S(2)}, u32[]{:S(2)}) %collective-permute-start.4) | collective-permute-done | bytes 229408 | tf_op jit(solution)/shard_map/ppermute | solution.py:30
  36.8 10.5 %collective-permute-done.5 = f32[56,1024]{1,0:T(8,128)S(1)} collective-permute-done((f32[56,1024]{1,0:T(8,128)S(1)}, f32[56,1024]{1,0:T(8,128)S(1)}, u32[]{:S(2)}, u32[]{:S(2)}) %collective-permute-start.5) | collective-permute-done | bytes 229408 | tf_op jit(solution)/shard_map/ppermute | solution.py:30
  47.4 0.1 multiply_reduce_fusion.1
  47.5 0.1 constant_dynamic-update-slice_fusion.4
  47.6 1.3 %collective-permute-start.7 = (bf16[56,1024]{1,0:T(8,128)(2,1)S(1)}, bf16[56,1024]{1,0:T(8,128)(2,1)S(1)}, u32[]{:S(2)}, u32[]{:S(2)}) collective-permute-start(bf16[56,1024]{1,0:T(8,128)(2,1)S(1)} %get-tuple-element.5), channel_id=1, source_target_pairs={{0,2},{1,3},{2,0},{3,1},{4,6},{5,7},{6,4},{7,5},{8,10},{9,11},{10,... | collective-permute-start | bytes 344072 | tf_op jit(solution)/shard_map/ppermute | solution.py:30
  48.9 0.8 collective-permute-start.8
  49.8 1.4 %collective-permute-start.9 = (bf16[56,1024]{1,0:T(8,128)(2,1)S(1)}, bf16[56,1024]{1,0:T(8,128)(2,1)S(1)}, u32[]{:S(2)}, u32[]{:S(2)}) collective-permute-start(bf16[56,1024]{1,0:T(8,128)(2,1)S(1)} %get-tuple-element.5), channel_id=1, source_target_pairs={{0,6},{1,7},{2,4},{3,5},{4,2},{5,3},{6,0},{7,1},{8,14},{9,15},{10,... | collective-permute-start | bytes 344072 | tf_op jit(solution)/shard_map/ppermute | solution.py:30
  51.2 1.3 %collective-permute-done.7 = bf16[56,1024]{1,0:T(8,128)(2,1)S(1)} collective-permute-done((bf16[56,1024]{1,0:T(8,128)(2,1)S(1)}, bf16[56,1024]{1,0:T(8,128)(2,1)S(1)}, u32[]{:S(2)}, u32[]{:S(2)}) %collective-permute-start.7) | collective-permute-done | bytes 114720 | tf_op jit(solution)/shard_map/ppermute | solution.py:30
  52.5 1.2 %collective-permute-done.8 = bf16[56,1024]{1,0:T(8,128)(2,1)S(1)} collective-permute-done((bf16[56,1024]{1,0:T(8,128)(2,1)S(1)}, bf16[56,1024]{1,0:T(8,128)(2,1)S(1)}, u32[]{:S(2)}, u32[]{:S(2)}) %collective-permute-start.8) | collective-permute-done | bytes 114720 | tf_op jit(solution)/shard_map/ppermute | solution.py:30
  53.7 1.7 %collective-permute-done.9 = bf16[56,1024]{1,0:T(8,128)(2,1)S(1)} collective-permute-done((bf16[56,1024]{1,0:T(8,128)(2,1)S(1)}, bf16[56,1024]{1,0:T(8,128)(2,1)S(1)}, u32[]{:S(2)}, u32[]{:S(2)}) %collective-permute-start.9) | collective-permute-done | bytes 114720 | tf_op jit(solution)/shard_map/ppermute | solution.py:30
  55.5 0.1 collective-permute-start.10
  55.6 1.7 %collective-permute-done.10 = bf16[224,1024]{1,0:T(8,128)(2,1)S(1)} collective-permute-done((bf16[224,1024]{1,0:T(8,128)(2,1)S(1)}, bf16[224,1024]{1,0:T(8,128)(2,1)S(1)}, u32[]{:S(2)}, u32[]{:S(2)}) %collective-permute-start.10) | collective-permute-done | bytes 458784 | tf_op jit(solution)/shard_map/ppermute | solution.py:30
  57.4 1.3 %fusion.33 = (f32[1024]{0:T(1024)S(1)}, f32[1024,448]{0,1:T(8,128)S(1)}) fusion(bf16[1024,1024]{1,0:T(8,128)(2,1)S(1)} %copy-done.1, bf16[448,1024]{1,0:T(8,128)(2,1)S(1)} %constant_dynamic-update-slice_fusion, pred[448]{0:T(512)(128)(4,1)S(1)} %fusion.30), kind=kOutput, calls=%fused_computation.84 | convolution fusion | flops 940899328 | bytes 4854208 | tf_op jit(solution)/shard_map/dot_general | solution.py:99
  58.7 1.1 %fusion.6 = f32[448,1024]{1,0:T(8,128)S(1)} fusion(bf16[1024,1024]{1,0:T(8,128)(2,1)S(1)} %copy-done.1, f32[1024,448]{0,1:T(8,128)S(1)} %get-tuple-element.15, f32[1024]{0:T(1024)S(1)} %get-tuple-element.14), kind=kOutput, calls=%fused_computation.16 | convolution fusion | flops 940441600 | bytes 5771264 | tf_op jit(solution)/shard_map/dot_general | solution.py:84
  59.8 0.1 slice.59
  59.9 0.2 collective-permute-start.11
  60.1 2.3 %collective-permute-done.11 = f32[224,1024]{1,0:T(8,128)S(1)} collective-permute-done((f32[224,1024]{1,0:T(8,128)S(1)}, f32[224,1024]{1,0:T(8,128)S(1)}, u32[]{:S(2)}, u32[]{:S(2)}) %collective-permute-start.11) | collective-permute-done | bytes 917536 | tf_op jit(solution)/shard_map/ppermute | solution.py:30
  62.5 0.1 slice_add_fusion
  62.6 0.1 fusion.10
  62.6 1.6 %collective-permute-start.12 = (f16[56,1024]{1,0:T(8,128)(2,1)S(1)}, f16[56,1024]{1,0:T(8,128)(2,1)S(1)}, u32[]{:S(2)}, u32[]{:S(2)}) collective-permute-start(f16[56,1024]{1,0:T(8,128)(2,1)S(1)} %get-tuple-element.8), channel_id=1, source_target_pairs={{0,2},{1,3},{2,0},{3,1},{4,6},{5,7},{6,4},{7,5},{8,10},{9,11},{10,... | collective-permute-start | bytes 344072 | tf_op jit(solution)/shard_map/ppermute | solution.py:30
  64.2 0.5 collective-permute-start.13
  64.7 1.5 %collective-permute-start.14 = (f16[56,1024]{1,0:T(8,128)(2,1)S(1)}, f16[56,1024]{1,0:T(8,128)(2,1)S(1)}, u32[]{:S(2)}, u32[]{:S(2)}) collective-permute-start(f16[56,1024]{1,0:T(8,128)(2,1)S(1)} %get-tuple-element.9), channel_id=1, source_target_pairs={{0,6},{1,7},{2,4},{3,5},{4,2},{5,3},{6,0},{7,1},{8,14},{9,15},{10,... | collective-permute-start | bytes 344072 | tf_op jit(solution)/shard_map/ppermute | solution.py:30
  66.2 1.8 %collective-permute-done.12 = f16[56,1024]{1,0:T(8,128)(2,1)S(1)} collective-permute-done((f16[56,1024]{1,0:T(8,128)(2,1)S(1)}, f16[56,1024]{1,0:T(8,128)(2,1)S(1)}, u32[]{:S(2)}, u32[]{:S(2)}) %collective-permute-start.12) | collective-permute-done | bytes 114720 | tf_op jit(solution)/shard_map/ppermute | solution.py:30
  68.0 3.6 %collective-permute-done.13 = f16[56,1024]{1,0:T(8,128)(2,1)S(1)} collective-permute-done((f16[56,1024]{1,0:T(8,128)(2,1)S(1)}, f16[56,1024]{1,0:T(8,128)(2,1)S(1)}, u32[]{:S(2)}, u32[]{:S(2)}) %collective-permute-start.13) | collective-permute-done | bytes 114720 | tf_op jit(solution)/shard_map/ppermute | solution.py:30
  71.6 0.1 fusion.14
  71.7 3.3 %collective-permute-start.15 = (f16[56,1024]{1,0:T(8,128)(2,1)S(1)}, f16[56,1024]{1,0:T(8,128)(2,1)S(1)}, u32[]{:S(2)}, u32[]{:S(2)}) collective-permute-start(f16[56,1024]{1,0:T(8,128)(2,1)S(1)} %fusion.14), channel_id=1, source_target_pairs={{0,8},{1,9},{2,10},{3,11},{4,12},{5,13},{6,14},{7,15},{8,0},{9,1},... | collective-permute-start | bytes 344072 | tf_op jit(solution)/shard_map/ppermute | solution.py:30
  75.0 1.1 %collective-permute-start.16 = (f16[56,1024]{1,0:T(8,128)(2,1)S(1)}, f16[56,1024]{1,0:T(8,128)(2,1)S(1)}, u32[]{:S(2)}, u32[]{:S(2)}) collective-permute-start(f16[56,1024]{1,0:T(8,128)(2,1)S(1)} %fusion.14), channel_id=1, source_target_pairs={{0,16},{1,17},{2,18},{3,19},{4,20},{5,21},{6,22},{7,23},{8,24},{9,... | collective-permute-start | bytes 344072 | tf_op jit(solution)/shard_map/ppermute | solution.py:30
  76.1 1.4 %collective-permute-start.17 = (f16[56,1024]{1,0:T(8,128)(2,1)S(1)}, f16[56,1024]{1,0:T(8,128)(2,1)S(1)}, u32[]{:S(2)}, u32[]{:S(2)}) collective-permute-start(f16[56,1024]{1,0:T(8,128)(2,1)S(1)} %fusion.14), channel_id=1, source_target_pairs={{0,24},{1,25},{2,26},{3,27},{4,28},{5,29},{6,30},{7,31},{8,16},{9,... | collective-permute-start | bytes 344072 | tf_op jit(solution)/shard_map/ppermute | solution.py:30
  77.5 1.4 %collective-permute-done.15 = f16[56,1024]{1,0:T(8,128)(2,1)S(1)} collective-permute-done((f16[56,1024]{1,0:T(8,128)(2,1)S(1)}, f16[56,1024]{1,0:T(8,128)(2,1)S(1)}, u32[]{:S(2)}, u32[]{:S(2)}) %collective-permute-start.15) | collective-permute-done | bytes 114720 | tf_op jit(solution)/shard_map/ppermute | solution.py:30
  78.9 7.0 %collective-permute-done.16 = f16[56,1024]{1,0:T(8,128)(2,1)S(1)} collective-permute-done((f16[56,1024]{1,0:T(8,128)(2,1)S(1)}, f16[56,1024]{1,0:T(8,128)(2,1)S(1)}, u32[]{:S(2)}, u32[]{:S(2)}) %collective-permute-start.16) | collective-permute-done | bytes 114720 | tf_op jit(solution)/shard_map/ppermute | solution.py:30
  85.9 0.2 multiply_reduce_fusion
  86.0 0.1 constant_dynamic-update-slice_fusion.9
  86.1 0.1 collective-permute-start.18
  86.2 2.0 %collective-permute-start.19 = (bf16[56,1024]{1,0:T(8,128)(2,1)S(1)}, bf16[56,1024]{1,0:T(8,128)(2,1)S(1)}, u32[]{:S(2)}, u32[]{:S(2)}) collective-permute-start(bf16[56,1024]{1,0:T(8,128)(2,1)S(1)} %get-tuple-element.3), channel_id=1, source_target_pairs={{0,4},{1,5},{2,6},{3,7},{4,0},{5,1},{6,2},{7,3},{8,12},{9,13},{10,... | collective-permute-start | bytes 344072 | tf_op jit(solution)/shard_map/ppermute | solution.py:30
  88.2 1.5 %collective-permute-start.20 = (bf16[56,1024]{1,0:T(8,128)(2,1)S(1)}, bf16[56,1024]{1,0:T(8,128)(2,1)S(1)}, u32[]{:S(2)}, u32[]{:S(2)}) collective-permute-start(bf16[56,1024]{1,0:T(8,128)(2,1)S(1)} %get-tuple-element.3), channel_id=1, source_target_pairs={{0,6},{1,7},{2,4},{3,5},{4,2},{5,3},{6,0},{7,1},{8,14},{9,15},{10,... | collective-permute-start | bytes 344072 | tf_op jit(solution)/shard_map/ppermute | solution.py:30
  89.7 1.3 %collective-permute-done.18 = bf16[56,1024]{1,0:T(8,128)(2,1)S(1)} collective-permute-done((bf16[56,1024]{1,0:T(8,128)(2,1)S(1)}, bf16[56,1024]{1,0:T(8,128)(2,1)S(1)}, u32[]{:S(2)}, u32[]{:S(2)}) %collective-permute-start.18) | collective-permute-done | bytes 114720 | tf_op jit(solution)/shard_map/ppermute | solution.py:30
  91.0 0.1 collective-permute-done.19
  91.1 2.8 %collective-permute-done.20 = bf16[56,1024]{1,0:T(8,128)(2,1)S(1)} collective-permute-done((bf16[56,1024]{1,0:T(8,128)(2,1)S(1)}, bf16[56,1024]{1,0:T(8,128)(2,1)S(1)}, u32[]{:S(2)}, u32[]{:S(2)}) %collective-permute-start.20) | collective-permute-done | bytes 114720 | tf_op jit(solution)/shard_map/ppermute | solution.py:30
  93.9 0.8 pad_maximum_fusion.1
  94.8 2.1 %collective-permute-done.21 = bf16[224,1024]{1,0:T(8,128)(2,1)} collective-permute-done((bf16[224,1024]{1,0:T(8,128)(2,1)}, bf16[224,1024]{1,0:T(8,128)(2,1)}, u32[]{:S(2)}, u32[]{:S(2)}) %collective-permute-start.21) | collective-permute-done | bytes 458784 | tf_op jit(solution)/shard_map/ppermute | solution.py:30
  96.9 1.0 %constant_dynamic-update-slice_fusion.5 = bf16[448,1024]{1,0:T(8,128)(2,1)S(1)} fusion(bf16[448,1024]{1,0:T(8,128)(2,1)S(1)} %constant_dynamic-update-slice_fusion.6, bf16[224,1024]{1,0:T(8,128)(2,1)} %collective-permute-done.21), kind=kLoop, calls=%fused_computation.51 | loop fusion | bytes 917504 | tf_op jit(solution)/shard_map/concatenate | solution.py:67
  97.9 0.2 reverse_select_fusion.2
  98.2 0.2 reverse_select_fusion.1
  98.4 0.2 reverse_select_fusion
  98.7 1.1 %reshape.77 = bf16[400,1024]{1,0:T(8,128)(2,1)} reshape(bf16[4,2,1,50,1024]{4,3,1,0,2:T(8,128)(2,1)S(1)} %reverse_select_fusion) | data formatting | bytes 1638400 | tf_op jit(solution)/shard_map/reshape | solution.py:97
  99.8 2.2 %fusion.34 = (f32[1024]{0:T(1024)S(1)}, f32[1024,400]{0,1:T(8,128)S(1)}) fusion(bf16[1024,1024]{1,0:T(8,128)(2,1)S(1)} %copy-done.1, bf16[400,1024]{1,0:T(8,128)(2,1)} %reshape.77), kind=kOutput, calls=%fused_computation.85 | convolution fusion | flops 839678976 | bytes 4558848 | tf_op jit(solution)/shard_map/dot_general | solution.py:99
  102.0 1.4 %divide_multiply_fusion = f32[1024,400]{0,1:T(8,128)} fusion(f32[1024,400]{0,1:T(8,128)S(1)} %get-tuple-element.17, f32[1024]{0:T(1024)S(1)} %get-tuple-element.16), kind=kLoop, calls=%fused_computation.10 | loop fusion | flops 819200 | bytes 3280896 | tf_op jit(solution)/shard_map/mul | solution.py:112
  (26 shorter events, 0.3 us)
Async XLA Ops:
  0.6 2.2 %copy-start = (bf16[1024,1024]{1,0:T(8,128)(2,1)S(1)}, bf16[1024,1024]{1,0:T(8,128)(2,1)}, u32[]{:S(2)}) copy-start(bf16[1024,1024]{1,0:T(8,128)(2,1)} %param.2) | copy-start | bytes 6291460
  3.6 1.9 %copy-start.2 = (s32[1024]{0:T(1024)S(1)}, s32[1024]{0:T(1024)}, u32[]{:S(2)}) copy-start(s32[1024]{0:T(1024)} %param.3) | copy-start | bytes 12292
  8.4 2.7 %collective-permute-start = (f32[224,1024]{1,0:T(8,128)S(1)}, f32[224,1024]{1,0:T(8,128)S(1)}, u32[]{:S(2)}, u32[]{:S(2)}) collective-permute-start(f32[224,1024]{1,0:T(8,128)S(1)} %slice.53), channel_id=1, source_target_pairs={{0,1},{1,0},{2,3},{3,2},{4,5},{5,4},{6,7},{7,6},{8,9},{9,8},{10,11... | collective-permute-start | bytes 2752520 | tf_op jit(solution)/shard_map/ppermute | solution.py:30
  11.3 9.4 %collective-permute-start.1 = (f32[56,1024]{1,0:T(8,128)S(1)}, f32[56,1024]{1,0:T(8,128)S(1)}, u32[]{:S(2)}, u32[]{:S(2)}) collective-permute-start(f32[56,1024]{1,0:T(8,128)S(1)} %get-tuple-element.13), channel_id=1, source_target_pairs={{0,2},{1,3},{2,0},{3,1},{4,6},{5,7},{6,4},{7,5},{8,10},{9,11},{10,... | collective-permute-start | bytes 688136 | tf_op jit(solution)/shard_map/ppermute | solution.py:30
  14.2 12.3 %collective-permute-start.2 = (f32[56,1024]{1,0:T(8,128)S(1)}, f32[56,1024]{1,0:T(8,128)S(1)}, u32[]{:S(2)}, u32[]{:S(2)}) collective-permute-start(f32[56,1024]{1,0:T(8,128)S(1)} %get-tuple-element.12), channel_id=1, source_target_pairs={{0,4},{1,5},{2,6},{3,7},{4,0},{5,1},{6,2},{7,3},{8,12},{9,13},{10,... | collective-permute-start | bytes 688136 | tf_op jit(solution)/shard_map/ppermute | solution.py:30
  15.7 10.8 %collective-permute-start.3 = (f32[56,1024]{1,0:T(8,128)S(1)}, f32[56,1024]{1,0:T(8,128)S(1)}, u32[]{:S(2)}, u32[]{:S(2)}) collective-permute-start(f32[56,1024]{1,0:T(8,128)S(1)} %get-tuple-element.11), channel_id=1, source_target_pairs={{0,6},{1,7},{2,4},{3,5},{4,2},{5,3},{6,0},{7,1},{8,14},{9,15},{10,... | collective-permute-start | bytes 688136 | tf_op jit(solution)/shard_map/ppermute | solution.py:30
  26.5 30.9 %copy-start.1 = (bf16[1024,1024]{1,0:T(8,128)(2,1)S(1)}, bf16[1024,1024]{1,0:T(8,128)(2,1)}, u32[]{:S(2)}) copy-start(bf16[1024,1024]{1,0:T(8,128)(2,1)} %fusion.3) | copy-start | bytes 6291460
  26.5 10.3 %collective-permute-start.4 = (f32[56,1024]{1,0:T(8,128)S(1)}, f32[56,1024]{1,0:T(8,128)S(1)}, u32[]{:S(2)}, u32[]{:S(2)}) collective-permute-start(f32[56,1024]{1,0:T(8,128)S(1)} %fusion.17), channel_id=1, source_target_pairs={{0,8},{1,9},{2,10},{3,11},{4,12},{5,13},{6,14},{7,15},{8,0},{9,1},... | collective-permute-start | bytes 688136 | tf_op jit(solution)/shard_map/ppermute | solution.py:30
  28.2 19.2 %collective-permute-start.5 = (f32[56,1024]{1,0:T(8,128)S(1)}, f32[56,1024]{1,0:T(8,128)S(1)}, u32[]{:S(2)}, u32[]{:S(2)}) collective-permute-start(f32[56,1024]{1,0:T(8,128)S(1)} %fusion.17), channel_id=1, source_target_pairs={{0,16},{1,17},{2,18},{3,19},{4,20},{5,21},{6,22},{7,23},{8,24},{9,... | collective-permute-start | bytes 688136 | tf_op jit(solution)/shard_map/ppermute | solution.py:30
  30.8 16.6 %collective-permute-start.6 = (f32[56,1024]{1,0:T(8,128)S(1)}, f32[56,1024]{1,0:T(8,128)S(1)}, u32[]{:S(2)}, u32[]{:S(2)}) collective-permute-start(f32[56,1024]{1,0:T(8,128)S(1)} %fusion.17), channel_id=1, source_target_pairs={{0,24},{1,25},{2,26},{3,27},{4,28},{5,29},{6,30},{7,31},{8,16},{9,... | collective-permute-start | bytes 688136 | tf_op jit(solution)/shard_map/ppermute | solution.py:30
  47.6 4.9 %collective-permute-start.7 = (bf16[56,1024]{1,0:T(8,128)(2,1)S(1)}, bf16[56,1024]{1,0:T(8,128)(2,1)S(1)}, u32[]{:S(2)}, u32[]{:S(2)}) collective-permute-start(bf16[56,1024]{1,0:T(8,128)(2,1)S(1)} %get-tuple-element.5), channel_id=1, source_target_pairs={{0,2},{1,3},{2,0},{3,1},{4,6},{5,7},{6,4},{7,5},{8,10},{9,11},{10,... | collective-permute-start | bytes 344072 | tf_op jit(solution)/shard_map/ppermute | solution.py:30
  48.9 4.8 %collective-permute-start.8 = (bf16[56,1024]{1,0:T(8,128)(2,1)S(1)}, bf16[56,1024]{1,0:T(8,128)(2,1)S(1)}, u32[]{:S(2)}, u32[]{:S(2)}) collective-permute-start(bf16[56,1024]{1,0:T(8,128)(2,1)S(1)} %get-tuple-element.5), channel_id=1, source_target_pairs={{0,4},{1,5},{2,6},{3,7},{4,0},{5,1},{6,2},{7,3},{8,12},{9,13},{10,... | collective-permute-start | bytes 344072 | tf_op jit(solution)/shard_map/ppermute | solution.py:30
  49.8 5.7 %collective-permute-start.9 = (bf16[56,1024]{1,0:T(8,128)(2,1)S(1)}, bf16[56,1024]{1,0:T(8,128)(2,1)S(1)}, u32[]{:S(2)}, u32[]{:S(2)}) collective-permute-start(bf16[56,1024]{1,0:T(8,128)(2,1)S(1)} %get-tuple-element.5), channel_id=1, source_target_pairs={{0,6},{1,7},{2,4},{3,5},{4,2},{5,3},{6,0},{7,1},{8,14},{9,15},{10,... | collective-permute-start | bytes 344072 | tf_op jit(solution)/shard_map/ppermute | solution.py:30
  55.5 1.9 %collective-permute-start.10 = (bf16[224,1024]{1,0:T(8,128)(2,1)S(1)}, bf16[224,1024]{1,0:T(8,128)(2,1)S(1)}, u32[]{:S(2)}, u32[]{:S(2)}) collective-permute-start(bf16[224,1024]{1,0:T(8,128)(2,1)S(1)} %pad_maximum_fusion), channel_id=1, source_target_pairs={{0,1},{1,0},{2,3},{3,2},{4,5},{5,4},{6,7},{7,6},{8,9},{9,8},{10,11... | collective-permute-start | bytes 1376264 | tf_op jit(solution)/shard_map/ppermute | solution.py:30
  59.9 2.5 %collective-permute-start.11 = (f32[224,1024]{1,0:T(8,128)S(1)}, f32[224,1024]{1,0:T(8,128)S(1)}, u32[]{:S(2)}, u32[]{:S(2)}) collective-permute-start(f32[224,1024]{1,0:T(8,128)S(1)} %slice.59), channel_id=1, source_target_pairs={{0,1},{1,0},{2,3},{3,2},{4,5},{5,4},{6,7},{7,6},{8,9},{9,8},{10,11... | collective-permute-start | bytes 2752520 | tf_op jit(solution)/shard_map/ppermute | solution.py:30
  62.6 5.3 %collective-permute-start.12 = (f16[56,1024]{1,0:T(8,128)(2,1)S(1)}, f16[56,1024]{1,0:T(8,128)(2,1)S(1)}, u32[]{:S(2)}, u32[]{:S(2)}) collective-permute-start(f16[56,1024]{1,0:T(8,128)(2,1)S(1)} %get-tuple-element.8), channel_id=1, source_target_pairs={{0,2},{1,3},{2,0},{3,1},{4,6},{5,7},{6,4},{7,5},{8,10},{9,11},{10,... | collective-permute-start | bytes 344072 | tf_op jit(solution)/shard_map/ppermute | solution.py:30
  64.2 7.4 %collective-permute-start.13 = (f16[56,1024]{1,0:T(8,128)(2,1)S(1)}, f16[56,1024]{1,0:T(8,128)(2,1)S(1)}, u32[]{:S(2)}, u32[]{:S(2)}) collective-permute-start(f16[56,1024]{1,0:T(8,128)(2,1)S(1)} %get-tuple-element.10), channel_id=1, source_target_pairs={{0,4},{1,5},{2,6},{3,7},{4,0},{5,1},{6,2},{7,3},{8,12},{9,13},{10,... | collective-permute-start | bytes 344072 | tf_op jit(solution)/shard_map/ppermute | solution.py:30
  64.7 6.9 %collective-permute-start.14 = (f16[56,1024]{1,0:T(8,128)(2,1)S(1)}, f16[56,1024]{1,0:T(8,128)(2,1)S(1)}, u32[]{:S(2)}, u32[]{:S(2)}) collective-permute-start(f16[56,1024]{1,0:T(8,128)(2,1)S(1)} %get-tuple-element.9), channel_id=1, source_target_pairs={{0,6},{1,7},{2,4},{3,5},{4,2},{5,3},{6,0},{7,1},{8,14},{9,15},{10,... | collective-permute-start | bytes 344072 | tf_op jit(solution)/shard_map/ppermute | solution.py:30
  71.7 7.2 %collective-permute-start.15 = (f16[56,1024]{1,0:T(8,128)(2,1)S(1)}, f16[56,1024]{1,0:T(8,128)(2,1)S(1)}, u32[]{:S(2)}, u32[]{:S(2)}) collective-permute-start(f16[56,1024]{1,0:T(8,128)(2,1)S(1)} %fusion.14), channel_id=1, source_target_pairs={{0,8},{1,9},{2,10},{3,11},{4,12},{5,13},{6,14},{7,15},{8,0},{9,1},... | collective-permute-start | bytes 344072 | tf_op jit(solution)/shard_map/ppermute | solution.py:30
  75.0 10.9 %collective-permute-start.16 = (f16[56,1024]{1,0:T(8,128)(2,1)S(1)}, f16[56,1024]{1,0:T(8,128)(2,1)S(1)}, u32[]{:S(2)}, u32[]{:S(2)}) collective-permute-start(f16[56,1024]{1,0:T(8,128)(2,1)S(1)} %fusion.14), channel_id=1, source_target_pairs={{0,16},{1,17},{2,18},{3,19},{4,20},{5,21},{6,22},{7,23},{8,24},{9,... | collective-permute-start | bytes 344072 | tf_op jit(solution)/shard_map/ppermute | solution.py:30
  76.1 9.8 %collective-permute-start.17 = (f16[56,1024]{1,0:T(8,128)(2,1)S(1)}, f16[56,1024]{1,0:T(8,128)(2,1)S(1)}, u32[]{:S(2)}, u32[]{:S(2)}) collective-permute-start(f16[56,1024]{1,0:T(8,128)(2,1)S(1)} %fusion.14), channel_id=1, source_target_pairs={{0,24},{1,25},{2,26},{3,27},{4,28},{5,29},{6,30},{7,31},{8,16},{9,... | collective-permute-start | bytes 344072 | tf_op jit(solution)/shard_map/ppermute | solution.py:30
  86.1 4.9 %collective-permute-start.18 = (bf16[56,1024]{1,0:T(8,128)(2,1)S(1)}, bf16[56,1024]{1,0:T(8,128)(2,1)S(1)}, u32[]{:S(2)}, u32[]{:S(2)}) collective-permute-start(bf16[56,1024]{1,0:T(8,128)(2,1)S(1)} %get-tuple-element.3), channel_id=1, source_target_pairs={{0,2},{1,3},{2,0},{3,1},{4,6},{5,7},{6,4},{7,5},{8,10},{9,11},{10,... | collective-permute-start | bytes 344072 | tf_op jit(solution)/shard_map/ppermute | solution.py:30
  86.2 4.9 %collective-permute-start.19 = (bf16[56,1024]{1,0:T(8,128)(2,1)S(1)}, bf16[56,1024]{1,0:T(8,128)(2,1)S(1)}, u32[]{:S(2)}, u32[]{:S(2)}) collective-permute-start(bf16[56,1024]{1,0:T(8,128)(2,1)S(1)} %get-tuple-element.3), channel_id=1, source_target_pairs={{0,4},{1,5},{2,6},{3,7},{4,0},{5,1},{6,2},{7,3},{8,12},{9,13},{10,... | collective-permute-start | bytes 344072 | tf_op jit(solution)/shard_map/ppermute | solution.py:30
  88.2 5.7 %collective-permute-start.20 = (bf16[56,1024]{1,0:T(8,128)(2,1)S(1)}, bf16[56,1024]{1,0:T(8,128)(2,1)S(1)}, u32[]{:S(2)}, u32[]{:S(2)}) collective-permute-start(bf16[56,1024]{1,0:T(8,128)(2,1)S(1)} %get-tuple-element.3), channel_id=1, source_target_pairs={{0,6},{1,7},{2,4},{3,5},{4,2},{5,3},{6,0},{7,1},{8,14},{9,15},{10,... | collective-permute-start | bytes 344072 | tf_op jit(solution)/shard_map/ppermute | solution.py:30
  94.7 2.2 %collective-permute-start.21 = (bf16[224,1024]{1,0:T(8,128)(2,1)}, bf16[224,1024]{1,0:T(8,128)(2,1)}, u32[]{:S(2)}, u32[]{:S(2)}) collective-permute-start(bf16[224,1024]{1,0:T(8,128)(2,1)} %pad_maximum_fusion.1), channel_id=1, source_target_pairs={{0,1},{1,0},{2,3},{3,2},{4,5},{5,4},{6,7},{7,6},{8,9},{9,8},{10,11... | collective-permute-start | bytes 1376264 | tf_op jit(solution)/shard_map/ppermute | solution.py:30

commit v2 on v1

v2 whole, which is shorter than its diff:
```python
import math

import jax
import jax.numpy as jnp
from jax import lax
from jax.experimental import pallas as pl
from jax.experimental.pallas import tpu as pltpu
from jax.sharding import PartitionSpec as P

MODULES = 400
ITERS = 2


epsilon = 1e-05
sharpness = 30.0

AXIS = "genes"
BLOCKS = 8
ROW_TILE = 8
HALF_MAX = 60000.0


def swap(value, devices, bit):
    return lax.ppermute(value, AXIS, [(i, i ^ bit) for i in range(devices)])


def power_below(limit):
    return 2.0 ** math.floor(math.log2(limit))


def to_half(bound):
    down = power_below(HALF_MAX / bound)

    def encode(value):
        return (value * down).astype(jnp.float16)

    def decode(sent):
        return sent.astype(jnp.float32) * (1.0 / down)

    return encode, decode


def normalise(total):
    scale = lax.rsqrt(jnp.mean(total * total, axis=1, keepdims=True) + epsilon)
    return (total * scale).astype(jnp.bfloat16)


def four_sum(own, others):
    total = own + others[0]
    return total + (others[1] + others[2]) if len(others) == 3 else total


def spread(sent, devices, bit):
    steps = range(1, min(4, devices // bit))
    return [swap(sent, devices, bit * k) for k in steps]


def in_plane(kept, given, devices, encode, decode):
    rows = kept.shape[0] // 4
    kept, received = lax.optimization_barrier((kept, swap(given, devices, 1)))
    chip = kept + received
    others = [decode(swap(encode(chip[k * rows:(k + 1) * rows]), devices, 2 * k)) for k in range(1, 4)]
    return four_sum(chip[:rows], others)


def half_block(kept, given, devices, bound):
    total = in_plane(kept, given, devices, *to_half(2.0 * bound))
    bound = 8.0 * bound
    bit = 8
    while bit < devices:
        encode, decode = to_half(bound)
        sent = encode(total)
        others = spread(sent, devices, bit)
        total = four_sum(decode(sent), [decode(other) for other in others])
        bound = bound * (len(others) + 1)
        bit = bit * (len(others) + 1)
    return normalise(total)


def full_block(kept, given, devices, used):
    total = in_plane(kept, given, devices, lambda value: value, lambda value: value)
    rows, samples = total.shape
    bit = 8
    members = min(4, devices // bit)
    if members < 2:
        return normalise(total)
    part = -(-used // members)
    member = (lax.axis_index(AXIS) // bit) % members
    lanes = 128
    parts = jnp.pad(total, ((0, max(0, part * members - rows)), (0, 0)))[:part * members]
    parts = parts.reshape(members, part, samples // lanes, lanes)

    def part_of(k):
        return lax.dynamic_index_in_dim(parts, member ^ k, 0, keepdims=False)

    total = four_sum(part_of(0), [swap(part_of(k), devices, bit * k) for k in range(1, members)])
    rest = bit * members
    while rest < devices:
        others = spread(total, devices, rest)
        total = four_sum(total, others)
        rest = rest * (len(others) + 1)
    scale = lax.rsqrt(jnp.sum(total * total, axis=(1, 2), keepdims=True) * (1.0 / samples) + epsilon)
    mine = (total * scale).astype(jnp.bfloat16)
    pieces = jnp.stack([mine] + spread(mine, devices, bit))
    ordered = [lax.dynamic_index_in_dim(pieces, member ^ m, 0, keepdims=False) for m in range(members)]
    block = jnp.concatenate(ordered, axis=0)[:rows].reshape(-1, samples)
    return jnp.pad(block, ((0, rows - block.shape[0]), (0, 0)))


def gather_blocks(block, devices):
    half = jnp.concatenate([block] + [swap(block, devices, 2 * k) for k in range(1, 4)], axis=0)
    return half, swap(half, devices, 1)


CHUNKS = 4
KERNEL_BYTES = 24 << 20


def dot_tt(a, b):
    return lax.dot_general(a, b, (((1,), (1,)), ((), ())), preferred_element_type=jnp.float32)


def dot(a, b):
    return lax.dot_general(a, b, (((1,), (0,)), ((), ())), preferred_element_type=jnp.float32)


def slots(label, mine, rows):
    used = -(-MODULES // BLOCKS)
    block = jnp.zeros_like(label)
    for b in range(1, BLOCKS):
        block += jnp.where(label >= b * used, 1, 0)
    return (block ^ mine) * rows + (label - block * used)


def first_kernel(mine_ref, label_ref, expression_ref, standard_ref, given_ref, buffer, sems):
    genes, samples = standard_ref.shape
    size = genes // CHUNKS
    copies = [
        pltpu.make_async_copy(expression_ref.at[pl.ds(c * size, size)], buffer.at[pl.ds(c * size, size)], sems.at[c])
        for c in range(CHUNKS)
    ]
    for copy in copies:
        copy.start()
    slot = slots(label_ref[...], mine_ref[0], given_ref.shape[0] // (BLOCKS // 2)) - given_ref.shape[0]
    for c, copy in enumerate(copies):
        copy.wait()
        span = pl.ds(c * size, size)
        values = buffer[span, :].astype(jnp.float32)
        centre = jnp.sum(values, axis=1, keepdims=True) * (1.0 / samples)
        shifted = values - centre
        spread = jnp.sum(shifted * shifted, axis=1, keepdims=True) * (1.0 / samples)
        part = (shifted * lax.rsqrt(spread + epsilon)).astype(jnp.bfloat16)
        standard_ref[span, :] = part
        row = lax.broadcasted_iota(jnp.int32, (given_ref.shape[0], size), 0)
        weights = jnp.where(row == slot[:, c * size:(c + 1) * size], 1.0, 0.0).astype(jnp.bfloat16)
        if c == 0:
            given_ref[...] = dot(weights, part)
        else:
            given_ref[...] += dot(weights, part)


def raise_half(eigengenes, standard, start, mine):
    samples = standard.shape[1]
    rows = eigengenes.shape[0] // (BLOCKS // 2)
    used = -(-MODULES // BLOCKS)
    row = jnp.arange(eigengenes.shape[0], dtype=jnp.int32)
    number = ((start + row // rows) ^ mine) * used + row % rows
    real = (row % rows < used) & (number < MODULES)
    raised = jnp.exp(dot_tt(standard, eigengenes) * (sharpness / samples))
    return jnp.where(real[None, :], raised, 0.0)


def weigh(weights, standard):
    return lax.dot_general(weights, standard, (((0,), (0,)), ((), ())), preferred_element_type=jnp.float32)


def last_kernel(source_ref, mine_ref, other_ref, standard_ref, share_ref, eigen_ref):
    @pl.when(pl.program_id(0) == 0)
    def _():
        half = mine_ref.shape[0]
        column = lax.broadcasted_iota(jnp.int32, (MODULES, half), 1)
        rows = source_ref[...]
        first = jnp.where(column == rows, 1.0, 0.0).astype(jnp.bfloat16)
        second = jnp.where(column == rows - half, 1.0, 0.0).astype(jnp.bfloat16)
        picked = dot(first, mine_ref[...]) + dot(second, other_ref[...])
        eigen_ref[...] = picked.astype(jnp.bfloat16)

    genes, samples = standard_ref.shape
    size = genes // CHUNKS
    part = standard_ref[pl.ds(pl.multiple_of(pl.program_id(0) * size, size), size), :]
    raised = jnp.exp(dot_tt(eigen_ref[...], part) * (sharpness / samples))
    share_ref[...] = raised * (MODULES / jnp.sum(raised, axis=0, keepdims=True))


def on_chip(value):
    return pltpu.with_memory_space_constraint(value, pltpu.VMEM)


def in_vmem(count):
    return [pl.BlockSpec(memory_space=pltpu.VMEM)] * count


def shards(devices):
    def body(expression, labels):
        genes, samples = expression.shape
        used = -(-MODULES // BLOCKS)
        rows = -(-used // ROW_TILE) * ROW_TILE
        half = BLOCKS // 2 * rows
        place = lax.axis_index(AXIS)
        mine = ((place & 1) * 4 + ((place >> 1) & 3)).astype(jnp.int32)
        bound = genes * math.sqrt(samples) * 1.02
        f32 = jnp.float32

        module = jnp.arange(MODULES, dtype=jnp.int32)
        source = ((module // used) ^ mine) * rows + module % used

        standard, given = pl.pallas_call(
            first_kernel,
            out_shape=[pltpu.VMEM((genes, samples), jnp.bfloat16), pltpu.VMEM((half, samples), f32)],
            in_specs=[
                pl.BlockSpec(memory_space=pltpu.SMEM),
                pl.BlockSpec(memory_space=pltpu.VMEM),
                pl.BlockSpec(memory_space=pltpu.HBM),
            ],
            out_specs=in_vmem(2),
            scratch_shapes=[pltpu.VMEM((genes, samples), jnp.bfloat16), pltpu.SemaphoreType.DMA((CHUNKS,))],
            name="first",
                compiler_params=pltpu.CompilerParams(vmem_limit_bytes=KERNEL_BYTES),
        )(mine[None], labels[None, :], pltpu.with_memory_space_constraint(expression, pltpu.HBM))
        slot = slots(labels, mine, rows)
        column = jnp.arange(half, dtype=jnp.int32)
        kept = weigh((slot[:, None] == column[None, :]).astype(jnp.bfloat16), standard)
        for iteration in range(ITERS):
            last = iteration == ITERS - 1
            block = half_block(kept, given, devices, bound) if last else full_block(kept, given, devices, used)
            own, other = gather_blocks(block, devices)
            if not last:
                mine_raised = raise_half(own, standard, 0, mine)
                other_raised = raise_half(other, standard, BLOCKS // 2, mine)
                total = jnp.sum(mine_raised, axis=1, keepdims=True) + jnp.sum(other_raised, axis=1, keepdims=True)
                given = weigh((other_raised / total).astype(jnp.bfloat16), standard)
                kept = weigh((mine_raised / total).astype(jnp.bfloat16), standard)
        size = genes // CHUNKS
        shares, eigengenes = pl.pallas_call(
            last_kernel,
            out_shape=[
                jax.ShapeDtypeStruct((MODULES, genes), f32),
                jax.ShapeDtypeStruct((MODULES, samples), jnp.bfloat16),
            ],
            grid=(CHUNKS,),
            in_specs=[
                pl.BlockSpec((MODULES, 1), lambda c: (0, 0)),
            ] + in_vmem(3),
            out_specs=[
                pl.BlockSpec((MODULES, size), lambda c: (0, c)),
                pl.BlockSpec((MODULES, samples), lambda c: (0, 0)),
            ],
            name="last",
                compiler_params=pltpu.CompilerParams(vmem_limit_bytes=KERNEL_BYTES),
        )(source[:, None], on_chip(own), on_chip(other), on_chip(standard))
        return shares.T, eigengenes

    return body


def solution(mesh):
    placed = (P(AXIS, None), P(AXIS))
    return jax.shard_map(
        shards(mesh.shape[AXIS]), mesh=mesh, in_specs=placed, out_specs=(P(AXIS, None), P()), check_vma=False
    )
```

time: 104 us -> 91.3 us (0.88)
  waiting for transfers between devices: 57.6 us -> 47.2 us
  Pallas kernels: 0 us -> 6.52 us
  other arithmetic: 8.7 us -> 2.34 us
  matrix products: 7.44 us -> 4.03 us
  starting transfers between devices: 26.2 us -> 29.2 us
  local copies, waits for them, and re-layouts: 2.56 us -> 0.92 us
    ppermute x22 -> x25, waiting for transfers between devices: 57.6 us -> 47.2 us  [swap(): return lax.ppermute(value, AXIS, [(i, i ^ bit) for i in range(devices)])]
    pallas_call x0 -> x2, Pallas kernels: none -> 6.52 us  [the longest x1 3.55 us: body(): pl.pallas_call(last_kernel, out_shape=[jax.ShapeDtypeStruct((MODULES, gen...]
    dot_general x4 -> x5, matrix products: 7.44 us -> 4.03 us  [the longest x3 2.25 us: weigh(): lax.dot_general(weights, standard, (((0,), (0,)), ((), ())), preferred_el...]
    ppermute x22 -> x25, starting transfers between devices: 26.2 us -> 29.2 us  [swap(): return lax.ppermute(value, AXIS, [(i, i ^ bit) for i in range(devices)])]
    reduce_sum x4 -> x2, other arithmetic: 3.09 us -> 0.36 us  [the longest x1 0.19 us: full_block(): jnp.sum(total * total, axis=(1, 2), keepdims=True) * (1.0 / samples)]
    convert_element_type x3 -> x4, other arithmetic: 2.03 us -> 0.33 us  [the longest x2 0.15 us: encode(): return (value * down).astype(jnp.float16)]
    mul x5 -> x1, other arithmetic: 1.57 us -> 0.01 us  [normalise(): return (total * scale).astype(jnp.bfloat16)]
    reshape x1 -> x0, local copies, waits for them, and re-layouts: 1.12 us -> none  [body(): eigengenes = blocks.reshape(BLOCKS * used, samples)[:MODULES]]
  transfers between devices with their start and end apart: 22 -> 25, of which waited for: 18 -> 22; matrix products, arithmetic and copies ran while one was open for 0% -> 3% of each run, Pallas kernels for 0% -> 0%
where the time goes in v2:
time: 91.3 us; the launch traced here: 91.1 us
  waiting for transfers between devices  47.2 us (52%)
  starting transfers between devices  29.2 us (32%)
  Pallas kernels  6.52 us (7%)
  matrix products  4.03 us (4%)
  other arithmetic  2.34 us (3%)
  local copies, waits for them, and re-layouts  0.92 us (1%)
    ppermute x25, waiting for transfers between devices, swap(): return lax.ppermute(value, AXIS, [(i, i ^ bit) for i in range(devices)])  47.2 us
    ppermute x25, starting transfers between devices, swap(): return lax.ppermute(value, AXIS, [(i, i ^ bit) for i in range(devices)])  29.2 us
    pallas_call x1, Pallas kernels, body(): pl.pallas_call(last_kernel, out_shape=[jax.ShapeDtypeStruct((MODULES, gen...  3.55 us
    pallas_call x1, Pallas kernels, body(): pl.pallas_call(first_kernel, out_shape=[pltpu.VMEM((genes, samples), jnp....  2.97 us
    dot_general x3, matrix products, weigh(): lax.dot_general(weights, standard, (((0,), (0,)), ((), ())), preferred_el...  2.25 us
  transfers between devices with their start and end apart: 25, of which 22 were waited for; matrix products, arithmetic and copies ran while one was open for 3% of the time, Pallas kernels for 0%

profile of v2, /device:TPU:0, one launch (start us, length us, event | category | flops | bytes accessed | tf_op | source)
XLA Modules:
  0.0 91.1 jit_solution(10195834137072148063)
XLA Ops:
  0.6 0.7 copy-done
  1.3 3.0 %first.1 = (bf16[1024,1024]{1,0:T(8,128)(2,1)S(1)}, f32[224,1024]{1,0:T(8,128)S(1)}) custom-call(s32[1]{0:T(128)} %bitcast.mine_ref, s32[1,1024]{1,0:T(1,128)S(1)} %bitcast.49, bf16[1024,1024]{1,0:T(8,128)(2,1)} %expression_ref.1), custom_call_target="tpu_custom_call" | custom-call | tf_op jit(solution)/shard_map/first/pallas_call | solution.py:217
  4.3 0.6 collective-permute-start
  4.9 1.0 %fusion.4 = f32[224,1024]{1,0:T(8,128)S(1)} fusion(bf16[1024,1024]{1,0:T(8,128)(2,1)S(1)} %get-tuple-element.10.standard_ref, s32[1024]{0:T(1024)S(1)} %subtract_add_fusion), kind=kOutput, calls=%fused_computation.7 | convolution fusion | flops 469991424 | bytes 3018752 | tf_op jit(solution)/shard_map/dot_general | solution.py:174
  5.8 1.1 %collective-permute-done = f32[224,1024]{1,0:T(8,128)S(1)} collective-permute-done((f32[224,1024]{1,0:T(8,128)S(1)}, f32[224,1024]{1,0:T(8,128)S(1)}, u32[]{:S(2)}, u32[]{:S(2)}) %collective-permute-start) | collective-permute-done | bytes 917536 | tf_op jit(solution)/shard_map/ppermute | solution.py:24
  7.0 0.1 add.220
  7.1 0.1 fusion.37
  7.2 3.9 %collective-permute-start.3 = (f32[56,1024]{1,0:T(8,128)S(1)}, f32[56,1024]{1,0:T(8,128)S(1)}, u32[]{:S(2)}, u32[]{:S(2)}) collective-permute-start(f32[56,1024]{1,0:T(8,128)S(1)} %get-tuple-element.24), channel_id=1, source_target_pairs={{0,6},{1,7},{2,4},{3,5},{4,2},{5,3},{6,0},{7,1},{8,14},{9,15},{10,... | collective-permute-start | bytes 688136 | tf_op jit(solution)/shard_map/ppermute | solution.py:24
  11.1 0.5 collective-permute-start.2
  11.6 0.1 collective-permute-start.1
  11.7 5.9 %collective-permute-done.3 = f32[56,1024]{1,0:T(8,128)S(1)} collective-permute-done((f32[56,1024]{1,0:T(8,128)S(1)}, f32[56,1024]{1,0:T(8,128)S(1)}, u32[]{:S(2)}, u32[]{:S(2)}) %collective-permute-start.3) | collective-permute-done | bytes 229408 | tf_op jit(solution)/shard_map/ppermute | solution.py:24
  17.6 4.3 %collective-permute-done.2 = f32[56,1024]{1,0:T(8,128)S(1)} collective-permute-done((f32[56,1024]{1,0:T(8,128)S(1)}, f32[56,1024]{1,0:T(8,128)S(1)}, u32[]{:S(2)}, u32[]{:S(2)}) %collective-permute-start.2) | collective-permute-done | bytes 229408 | tf_op jit(solution)/shard_map/ppermute | solution.py:24
  21.9 0.4 collective-permute-done.1
  22.3 1.0 %fusion.24 = f32[52,1024]{1,0:T(8,128)S(1)} fusion(f32[56,1024]{1,0:T(8,128)S(1)} %collective-permute-done.3, f32[56,1024]{1,0:T(8,128)S(1)} %collective-permute-done.2, f32[56,1024]{1,0:T(8,128)} %collective-permute-done.1, f32[56,1024]{1,0:T(8,128)S(1)} %get-tuple-element.23), kind=kLoop, calls=%fused_computation.41 | loop fusion | flops 159744 | bytes 1064960 | tf_op jit(solution)/shard_map/add | solution.py:50
  23.4 1.6 %collective-permute-start.4 = (f32[13,8,128]{2,1,0:T(8,128)S(1)}, f32[13,8,128]{2,1,0:T(8,128)S(1)}, u32[]{:S(2)}, u32[]{:S(2)}) collective-permute-start(f32[13,8,128]{2,1,0:T(8,128)S(1)} %get-tuple-element.27), channel_id=1, source_target_pairs={{0,8},{1,9},{2,10},{3,11},{4,12},{5,13},{6,14},{7,15},{8,0},{9,1},... | collective-permute-start | bytes 159752 | tf_op jit(solution)/shard_map/ppermute | solution.py:24
  25.0 2.5 %collective-permute-start.6 = (f32[13,8,128]{2,1,0:T(8,128)S(1)}, f32[13,8,128]{2,1,0:T(8,128)S(1)}, u32[]{:S(2)}, u32[]{:S(2)}) collective-permute-start(f32[13,8,128]{2,1,0:T(8,128)S(1)} %get-tuple-element.28), channel_id=1, source_target_pairs={{0,24},{1,25},{2,26},{3,27},{4,28},{5,29},{6,30},{7,31},{8,16},{9,... | collective-permute-start | bytes 159752 | tf_op jit(solution)/shard_map/ppermute | solution.py:24
  27.5 0.1 collective-permute-start.5
  27.6 3.8 %collective-permute-done.6 = f32[13,8,128]{2,1,0:T(8,128)S(1)} collective-permute-done((f32[13,8,128]{2,1,0:T(8,128)S(1)}, f32[13,8,128]{2,1,0:T(8,128)S(1)}, u32[]{:S(2)}, u32[]{:S(2)}) %collective-permute-start.6) | collective-permute-done | bytes 53280 | tf_op jit(solution)/shard_map/ppermute | solution.py:24
  31.4 1.8 %collective-permute-done.5 = f32[13,8,128]{2,1,0:T(8,128)S(1)} collective-permute-done((f32[13,8,128]{2,1,0:T(8,128)S(1)}, f32[13,8,128]{2,1,0:T(8,128)S(1)}, u32[]{:S(2)}, u32[]{:S(2)}) %collective-permute-start.5) | collective-permute-done | bytes 53280 | tf_op jit(solution)/shard_map/ppermute | solution.py:24
  33.2 0.2 multiply_reduce_fusion.1
  33.4 0.1 multiply_convert_fusion.1
  33.5 0.9 %collective-permute-start.8 = (bf16[13,8,128]{2,1,0:T(8,128)(2,1)S(1)}, bf16[13,8,128]{2,1,0:T(8,128)(2,1)S(1)}, u32[]{:S(2)}, u32[]{:S(2)}) collective-permute-start(bf16[13,8,128]{2,1,0:T(8,128)(2,1)S(1)} %multiply_convert_fusion.1), channel_id=1, source_target_pairs={{0,16},{1,17},{2,18},{3,19},{4,20},{5,21},{6,22},{7,23},{8,24},{9,... | collective-permute-start | bytes 79880 | tf_op jit(solution)/shard_map/ppermute | solution.py:24
  34.4 2.0 %collective-permute-start.7 = (bf16[13,8,128]{2,1,0:T(8,128)(2,1)S(1)}, bf16[13,8,128]{2,1,0:T(8,128)(2,1)S(1)}, u32[]{:S(2)}, u32[]{:S(2)}) collective-permute-start(bf16[13,8,128]{2,1,0:T(8,128)(2,1)S(1)} %multiply_convert_fusion.1), channel_id=1, source_target_pairs={{0,8},{1,9},{2,10},{3,11},{4,12},{5,13},{6,14},{7,15},{8,0},{9,1},... | collective-permute-start | bytes 79880 | tf_op jit(solution)/shard_map/ppermute | solution.py:24
  36.4 1.5 %collective-permute-start.9 = (bf16[13,8,128]{2,1,0:T(8,128)(2,1)S(1)}, bf16[13,8,128]{2,1,0:T(8,128)(2,1)S(1)}, u32[]{:S(2)}, u32[]{:S(2)}) collective-permute-start(bf16[13,8,128]{2,1,0:T(8,128)(2,1)S(1)} %multiply_convert_fusion.1), channel_id=1, source_target_pairs={{0,24},{1,25},{2,26},{3,27},{4,28},{5,29},{6,30},{7,31},{8,16},{9,... | collective-permute-start | bytes 79880 | tf_op jit(solution)/shard_map/ppermute | solution.py:24
  38.0 0.1 fusion.46
  38.0 0.4 collective-permute-done.8
  38.4 0.1 collective-permute-done.7
  38.6 3.5 %collective-permute-done.9 = bf16[13,8,128]{2,1,0:T(8,128)(2,1)S(1)} collective-permute-done((bf16[13,8,128]{2,1,0:T(8,128)(2,1)S(1)}, bf16[13,8,128]{2,1,0:T(8,128)(2,1)S(1)}, u32[]{:S(2)}, u32[]{:S(2)}) %collective-permute-start.9) | collective-permute-done | bytes 26656 | tf_op jit(solution)/shard_map/ppermute | solution.py:24
  42.3 1.1 %collective-permute-start.12 = (bf16[56,1024]{1,0:T(8,128)(2,1)S(1)}, bf16[56,1024]{1,0:T(8,128)(2,1)S(1)}, u32[]{:S(2)}, u32[]{:S(2)}) collective-permute-start(bf16[56,1024]{1,0:T(8,128)(2,1)S(1)} %fusion.33), channel_id=1, source_target_pairs={{0,6},{1,7},{2,4},{3,5},{4,2},{5,3},{6,0},{7,1},{8,14},{9,15},{10,... | collective-permute-start | bytes 344072 | tf_op jit(solution)/shard_map/ppermute | solution.py:24
  43.4 1.9 %collective-permute-start.11 = (bf16[56,1024]{1,0:T(8,128)(2,1)S(1)}, bf16[56,1024]{1,0:T(8,128)(2,1)S(1)}, u32[]{:S(2)}, u32[]{:S(2)}) collective-permute-start(bf16[56,1024]{1,0:T(8,128)(2,1)S(1)} %fusion.33), channel_id=1, source_target_pairs={{0,4},{1,5},{2,6},{3,7},{4,0},{5,1},{6,2},{7,3},{8,12},{9,13},{10,... | collective-permute-start | bytes 344072 | tf_op jit(solution)/shard_map/ppermute | solution.py:24
  45.3 0.5 collective-permute-start.10
  45.9 2.3 %collective-permute-done.12 = bf16[56,1024]{1,0:T(8,128)(2,1)S(1)} collective-permute-done((bf16[56,1024]{1,0:T(8,128)(2,1)S(1)}, bf16[56,1024]{1,0:T(8,128)(2,1)S(1)}, u32[]{:S(2)}, u32[]{:S(2)}) %collective-permute-start.12) | collective-permute-done | bytes 114720 | tf_op jit(solution)/shard_map/ppermute | solution.py:24
  48.2 1.1 %collective-permute-done.11 = bf16[56,1024]{1,0:T(8,128)(2,1)S(1)} collective-permute-done((bf16[56,1024]{1,0:T(8,128)(2,1)S(1)}, bf16[56,1024]{1,0:T(8,128)(2,1)S(1)}, u32[]{:S(2)}, u32[]{:S(2)}) %collective-permute-start.11) | collective-permute-done | bytes 114720 | tf_op jit(solution)/shard_map/ppermute | solution.py:24
  49.3 0.8 collective-permute-done.10
  50.3 0.9 fusion.38
  51.2 0.9 collective-permute-done.13
  52.0 0.9 fusion.39
  53.0 0.7 fusion.7
  53.6 0.2 collective-permute-start.14
  53.8 0.6 fusion.6
  54.5 1.7 %collective-permute-done.14 = f32[224,1024]{1,0:T(8,128)S(1)} collective-permute-done((f32[224,1024]{1,0:T(8,128)S(1)}, f32[224,1024]{1,0:T(8,128)S(1)}, u32[]{:S(2)}, u32[]{:S(2)}) %collective-permute-start.14) | collective-permute-done | bytes 917536 | tf_op jit(solution)/shard_map/ppermute | solution.py:24
  56.2 0.1 add.237
  56.4 0.7 collective-permute-start.15
  57.1 1.4 %collective-permute-start.17 = (f16[56,1024]{1,0:T(8,128)(2,1)S(1)}, f16[56,1024]{1,0:T(8,128)(2,1)S(1)}, u32[]{:S(2)}, u32[]{:S(2)}) collective-permute-start(f16[56,1024]{1,0:T(8,128)(2,1)S(1)} %get-tuple-element.21), channel_id=1, source_target_pairs={{0,6},{1,7},{2,4},{3,5},{4,2},{5,3},{6,0},{7,1},{8,14},{9,15},{10,... | collective-permute-start | bytes 344072 | tf_op jit(solution)/shard_map/ppermute | solution.py:24
  58.5 1.4 %collective-permute-start.16 = (f16[56,1024]{1,0:T(8,128)(2,1)S(1)}, f16[56,1024]{1,0:T(8,128)(2,1)S(1)}, u32[]{:S(2)}, u32[]{:S(2)}) collective-permute-start(f16[56,1024]{1,0:T(8,128)(2,1)S(1)} %get-tuple-element.22), channel_id=1, source_target_pairs={{0,4},{1,5},{2,6},{3,7},{4,0},{5,1},{6,2},{7,3},{8,12},{9,13},{10,... | collective-permute-start | bytes 344072 | tf_op jit(solution)/shard_map/ppermute | solution.py:24
  59.9 2.5 %collective-permute-done.15 = f16[56,1024]{1,0:T(8,128)(2,1)S(1)} collective-permute-done((f16[56,1024]{1,0:T(8,128)(2,1)S(1)}, f16[56,1024]{1,0:T(8,128)(2,1)S(1)}, u32[]{:S(2)}, u32[]{:S(2)}) %collective-permute-start.15) | collective-permute-done | bytes 114720 | tf_op jit(solution)/shard_map/ppermute | solution.py:24
  62.5 1.8 %collective-permute-done.17 = f16[56,1024]{1,0:T(8,128)(2,1)S(1)} collective-permute-done((f16[56,1024]{1,0:T(8,128)(2,1)S(1)}, f16[56,1024]{1,0:T(8,128)(2,1)S(1)}, u32[]{:S(2)}, u32[]{:S(2)}) %collective-permute-start.17) | collective-permute-done | bytes 114720 | tf_op jit(solution)/shard_map/ppermute | solution.py:24
  64.2 1.4 %collective-permute-done.16 = f16[56,1024]{1,0:T(8,128)(2,1)S(1)} collective-permute-done((f16[56,1024]{1,0:T(8,128)(2,1)S(1)}, f16[56,1024]{1,0:T(8,128)(2,1)S(1)}, u32[]{:S(2)}, u32[]{:S(2)}) %collective-permute-start.16) | collective-permute-done | bytes 114720 | tf_op jit(solution)/shard_map/ppermute | solution.py:24
  65.6 0.1 fusion.19
  65.7 1.5 %collective-permute-start.20 = (f16[56,1024]{1,0:T(8,128)(2,1)S(1)}, f16[56,1024]{1,0:T(8,128)(2,1)S(1)}, u32[]{:S(2)}, u32[]{:S(2)}) collective-permute-start(f16[56,1024]{1,0:T(8,128)(2,1)S(1)} %fusion.19), channel_id=1, source_target_pairs={{0,24},{1,25},{2,26},{3,27},{4,28},{5,29},{6,30},{7,31},{8,16},{9,... | collective-permute-start | bytes 344072 | tf_op jit(solution)/shard_map/ppermute | solution.py:24
  67.2 2.9 %collective-permute-start.18 = (f16[56,1024]{1,0:T(8,128)(2,1)S(1)}, f16[56,1024]{1,0:T(8,128)(2,1)S(1)}, u32[]{:S(2)}, u32[]{:S(2)}) collective-permute-start(f16[56,1024]{1,0:T(8,128)(2,1)S(1)} %fusion.19), channel_id=1, source_target_pairs={{0,8},{1,9},{2,10},{3,11},{4,12},{5,13},{6,14},{7,15},{8,0},{9,1},... | collective-permute-start | bytes 344072 | tf_op jit(solution)/shard_map/ppermute | solution.py:24
  70.1 3.5 %collective-permute-done.20 = f16[56,1024]{1,0:T(8,128)(2,1)S(1)} collective-permute-done((f16[56,1024]{1,0:T(8,128)(2,1)S(1)}, f16[56,1024]{1,0:T(8,128)(2,1)S(1)}, u32[]{:S(2)}, u32[]{:S(2)}) %collective-permute-start.20) | collective-permute-done | bytes 114720 | tf_op jit(solution)/shard_map/ppermute | solution.py:24
  73.6 3.2 %collective-permute-done.19 = f16[56,1024]{1,0:T(8,128)(2,1)S(1)} collective-permute-done((f16[56,1024]{1,0:T(8,128)(2,1)S(1)}, f16[56,1024]{1,0:T(8,128)(2,1)S(1)}, u32[]{:S(2)}, u32[]{:S(2)}) %collective-permute-start.19) | collective-permute-done | bytes 114720 | tf_op jit(solution)/shard_map/ppermute | solution.py:24
  76.9 0.2 multiply_reduce_fusion
  77.0 0.1 multiply_convert_fusion
  77.1 1.6 %collective-permute-start.23 = (bf16[56,1024]{1,0:T(8,128)(2,1)S(1)}, bf16[56,1024]{1,0:T(8,128)(2,1)S(1)}, u32[]{:S(2)}, u32[]{:S(2)}) collective-permute-start(bf16[56,1024]{1,0:T(8,128)(2,1)S(1)} %multiply_convert_fusion), channel_id=1, source_target_pairs={{0,6},{1,7},{2,4},{3,5},{4,2},{5,3},{6,0},{7,1},{8,14},{9,15},{10,... | collective-permute-start | bytes 344072 | tf_op jit(solution)/shard_map/ppermute | solution.py:24
  78.7 1.3 %collective-permute-start.22 = (bf16[56,1024]{1,0:T(8,128)(2,1)S(1)}, bf16[56,1024]{1,0:T(8,128)(2,1)S(1)}, u32[]{:S(2)}, u32[]{:S(2)}) collective-permute-start(bf16[56,1024]{1,0:T(8,128)(2,1)S(1)} %multiply_convert_fusion), channel_id=1, source_target_pairs={{0,4},{1,5},{2,6},{3,7},{4,0},{5,1},{6,2},{7,3},{8,12},{9,13},{10,... | collective-permute-start | bytes 344072 | tf_op jit(solution)/shard_map/ppermute | solution.py:24
  80.0 0.7 collective-permute-start.21
  80.7 3.4 %collective-permute-done.23 = bf16[56,1024]{1,0:T(8,128)(2,1)S(1)} collective-permute-done((bf16[56,1024]{1,0:T(8,128)(2,1)S(1)}, bf16[56,1024]{1,0:T(8,128)(2,1)S(1)}, u32[]{:S(2)}, u32[]{:S(2)}) %collective-permute-start.23) | collective-permute-done | bytes 114720 | tf_op jit(solution)/shard_map/ppermute | solution.py:24
  84.1 1.5 %collective-permute-done.22 = bf16[56,1024]{1,0:T(8,128)(2,1)S(1)} collective-permute-done((bf16[56,1024]{1,0:T(8,128)(2,1)S(1)}, bf16[56,1024]{1,0:T(8,128)(2,1)S(1)}, u32[]{:S(2)}, u32[]{:S(2)}) %collective-permute-start.22) | collective-permute-done | bytes 114720 | tf_op jit(solution)/shard_map/ppermute | solution.py:24
  85.7 0.1 collective-permute-start.24
  85.8 0.1 fusion.29.source_ref
  85.9 1.7 %collective-permute-done.24.other_ref = bf16[224,1024]{1,0:T(8,128)(2,1)S(1)} collective-permute-done((bf16[224,1024]{1,0:T(8,128)(2,1)S(1)}, bf16[224,1024]{1,0:T(8,128)(2,1)S(1)}, u32[]{:S(2)}, u32[]{:S(2)}) %collective-permute-start.24) | collective-permute-done | bytes 458784 | tf_op jit(solution)/shard_map/ppermute | solution.py:24
  87.6 3.5 %last.1 = (f32[400,1024]{1,0:T(8,128)}, bf16[400,1024]{1,0:T(8,128)(2,1)}) custom-call(s32[400,1]{1,0:T(8,128)S(1)} %fusion.29.source_ref, bf16[224,1024]{1,0:T(8,128)(2,1)S(1)} %pad_maximum_fusion.1.mine_ref, bf16[224,1024]{1,0:T(8,128)(2,1)S(1)} %collective-permute-done.24.other_ref, bf16[1024,1024]{1,0:T(8,128)(2,1)S(1)} %get-tuple-element.10.standard_ref), custom_call_target="tpu_custom_call" | custom-call | tf_op jit(solution)/shard_map/last/pallas_call | solution.py:244
  (29 shorter events, 0.5 us)
Async XLA Ops:
  0.6 0.7 copy-start
  4.3 2.7 %collective-permute-start = (f32[224,1024]{1,0:T(8,128)S(1)}, f32[224,1024]{1,0:T(8,128)S(1)}, u32[]{:S(2)}, u32[]{:S(2)}) collective-permute-start(f32[224,1024]{1,0:T(8,128)S(1)} %get-tuple-element.11), channel_id=1, source_target_pairs={{0,1},{1,0},{2,3},{3,2},{4,5},{5,4},{6,7},{7,6},{8,9},{9,8},{10,11... | collective-permute-start | bytes 2752520 | tf_op jit(solution)/shard_map/ppermute | solution.py:24
  7.2 10.4 %collective-permute-start.3 = (f32[56,1024]{1,0:T(8,128)S(1)}, f32[56,1024]{1,0:T(8,128)S(1)}, u32[]{:S(2)}, u32[]{:S(2)}) collective-permute-start(f32[56,1024]{1,0:T(8,128)S(1)} %get-tuple-element.24), channel_id=1, source_target_pairs={{0,6},{1,7},{2,4},{3,5},{4,2},{5,3},{6,0},{7,1},{8,14},{9,15},{10,... | collective-permute-start | bytes 688136 | tf_op jit(solution)/shard_map/ppermute | solution.py:24
  11.1 10.8 %collective-permute-start.2 = (f32[56,1024]{1,0:T(8,128)S(1)}, f32[56,1024]{1,0:T(8,128)S(1)}, u32[]{:S(2)}, u32[]{:S(2)}) collective-permute-start(f32[56,1024]{1,0:T(8,128)S(1)} %get-tuple-element.25), channel_id=1, source_target_pairs={{0,4},{1,5},{2,6},{3,7},{4,0},{5,1},{6,2},{7,3},{8,12},{9,13},{10,... | collective-permute-start | bytes 688136 | tf_op jit(solution)/shard_map/ppermute | solution.py:24
  11.6 10.7 %collective-permute-start.1 = (f32[56,1024]{1,0:T(8,128)S(1)}, f32[56,1024]{1,0:T(8,128)}, u32[]{:S(2)}, u32[]{:S(2)}) collective-permute-start(f32[56,1024]{1,0:T(8,128)S(1)} %get-tuple-element.26), channel_id=1, source_target_pairs={{0,2},{1,3},{2,0},{3,1},{4,6},{5,7},{6,4},{7,5},{8,10},{9,11},{10,... | collective-permute-start | bytes 688136 | tf_op jit(solution)/shard_map/ppermute | solution.py:24
  23.4 4.2 %collective-permute-start.4 = (f32[13,8,128]{2,1,0:T(8,128)S(1)}, f32[13,8,128]{2,1,0:T(8,128)S(1)}, u32[]{:S(2)}, u32[]{:S(2)}) collective-permute-start(f32[13,8,128]{2,1,0:T(8,128)S(1)} %get-tuple-element.27), channel_id=1, source_target_pairs={{0,8},{1,9},{2,10},{3,11},{4,12},{5,13},{6,14},{7,15},{8,0},{9,1},... | collective-permute-start | bytes 159752 | tf_op jit(solution)/shard_map/ppermute | solution.py:24
  25.0 6.4 %collective-permute-start.6 = (f32[13,8,128]{2,1,0:T(8,128)S(1)}, f32[13,8,128]{2,1,0:T(8,128)S(1)}, u32[]{:S(2)}, u32[]{:S(2)}) collective-permute-start(f32[13,8,128]{2,1,0:T(8,128)S(1)} %get-tuple-element.28), channel_id=1, source_target_pairs={{0,24},{1,25},{2,26},{3,27},{4,28},{5,29},{6,30},{7,31},{8,16},{9,... | collective-permute-start | bytes 159752 | tf_op jit(solution)/shard_map/ppermute | solution.py:24
  27.5 5.7 %collective-permute-start.5 = (f32[13,8,128]{2,1,0:T(8,128)S(1)}, f32[13,8,128]{2,1,0:T(8,128)S(1)}, u32[]{:S(2)}, u32[]{:S(2)}) collective-permute-start(f32[13,8,128]{2,1,0:T(8,128)S(1)} %get-tuple-element.29), channel_id=1, source_target_pairs={{0,16},{1,17},{2,18},{3,19},{4,20},{5,21},{6,22},{7,23},{8,24},{9,... | collective-permute-start | bytes 159752 | tf_op jit(solution)/shard_map/ppermute | solution.py:24
  33.5 4.9 %collective-permute-start.8 = (bf16[13,8,128]{2,1,0:T(8,128)(2,1)S(1)}, bf16[13,8,128]{2,1,0:T(8,128)(2,1)S(1)}, u32[]{:S(2)}, u32[]{:S(2)}) collective-permute-start(bf16[13,8,128]{2,1,0:T(8,128)(2,1)S(1)} %multiply_convert_fusion.1), channel_id=1, source_target_pairs={{0,16},{1,17},{2,18},{3,19},{4,20},{5,21},{6,22},{7,23},{8,24},{9,... | collective-permute-start | bytes 79880 | tf_op jit(solution)/shard_map/ppermute | solution.py:24
  34.4 4.1 %collective-permute-start.7 = (bf16[13,8,128]{2,1,0:T(8,128)(2,1)S(1)}, bf16[13,8,128]{2,1,0:T(8,128)(2,1)S(1)}, u32[]{:S(2)}, u32[]{:S(2)}) collective-permute-start(bf16[13,8,128]{2,1,0:T(8,128)(2,1)S(1)} %multiply_convert_fusion.1), channel_id=1, source_target_pairs={{0,8},{1,9},{2,10},{3,11},{4,12},{5,13},{6,14},{7,15},{8,0},{9,1},... | collective-permute-start | bytes 79880 | tf_op jit(solution)/shard_map/ppermute | solution.py:24
  36.4 5.6 %collective-permute-start.9 = (bf16[13,8,128]{2,1,0:T(8,128)(2,1)S(1)}, bf16[13,8,128]{2,1,0:T(8,128)(2,1)S(1)}, u32[]{:S(2)}, u32[]{:S(2)}) collective-permute-start(bf16[13,8,128]{2,1,0:T(8,128)(2,1)S(1)} %multiply_convert_fusion.1), channel_id=1, source_target_pairs={{0,24},{1,25},{2,26},{3,27},{4,28},{5,29},{6,30},{7,31},{8,16},{9,... | collective-permute-start | bytes 79880 | tf_op jit(solution)/shard_map/ppermute | solution.py:24
  42.3 5.9 %collective-permute-start.12 = (bf16[56,1024]{1,0:T(8,128)(2,1)S(1)}, bf16[56,1024]{1,0:T(8,128)(2,1)S(1)}, u32[]{:S(2)}, u32[]{:S(2)}) collective-permute-start(bf16[56,1024]{1,0:T(8,128)(2,1)S(1)} %fusion.33), channel_id=1, source_target_pairs={{0,6},{1,7},{2,4},{3,5},{4,2},{5,3},{6,0},{7,1},{8,14},{9,15},{10,... | collective-permute-start | bytes 344072 | tf_op jit(solution)/shard_map/ppermute | solution.py:24
  43.4 5.9 %collective-permute-start.11 = (bf16[56,1024]{1,0:T(8,128)(2,1)S(1)}, bf16[56,1024]{1,0:T(8,128)(2,1)S(1)}, u32[]{:S(2)}, u32[]{:S(2)}) collective-permute-start(bf16[56,1024]{1,0:T(8,128)(2,1)S(1)} %fusion.33), channel_id=1, source_target_pairs={{0,4},{1,5},{2,6},{3,7},{4,0},{5,1},{6,2},{7,3},{8,12},{9,13},{10,... | collective-permute-start | bytes 344072 | tf_op jit(solution)/shard_map/ppermute | solution.py:24
  45.3 4.8 %collective-permute-start.10 = (bf16[56,1024]{1,0:T(8,128)(2,1)S(1)}, bf16[56,1024]{1,0:T(8,128)(2,1)S(1)}, u32[]{:S(2)}, u32[]{:S(2)}) collective-permute-start(bf16[56,1024]{1,0:T(8,128)(2,1)S(1)} %fusion.33), channel_id=1, source_target_pairs={{0,2},{1,3},{2,0},{3,1},{4,6},{5,7},{6,4},{7,5},{8,10},{9,11},{10,... | collective-permute-start | bytes 344072 | tf_op jit(solution)/shard_map/ppermute | solution.py:24
  50.2 1.9 %collective-permute-start.13 = (bf16[224,1024]{1,0:T(8,128)(2,1)S(1)}, bf16[224,1024]{1,0:T(8,128)(2,1)S(1)}, u32[]{:S(2)}, u32[]{:S(2)}) collective-permute-start(bf16[224,1024]{1,0:T(8,128)(2,1)S(1)} %pad_maximum_fusion), channel_id=1, source_target_pairs={{0,1},{1,0},{2,3},{3,2},{4,5},{5,4},{6,7},{7,6},{8,9},{9,8},{10,11... | collective-permute-start | bytes 1376264 | tf_op jit(solution)/shard_map/ppermute | solution.py:24
  53.6 2.5 %collective-permute-start.14 = (f32[224,1024]{1,0:T(8,128)S(1)}, f32[224,1024]{1,0:T(8,128)S(1)}, u32[]{:S(2)}, u32[]{:S(2)}) collective-permute-start(f32[224,1024]{1,0:T(8,128)S(1)} %fusion.7), channel_id=1, source_target_pairs={{0,1},{1,0},{2,3},{3,2},{4,5},{5,4},{6,7},{7,6},{8,9},{9,8},{10,11... | collective-permute-start | bytes 2752520 | tf_op jit(solution)/shard_map/ppermute | solution.py:24
  56.4 6.1 %collective-permute-start.15 = (f16[56,1024]{1,0:T(8,128)(2,1)S(1)}, f16[56,1024]{1,0:T(8,128)(2,1)S(1)}, u32[]{:S(2)}, u32[]{:S(2)}) collective-permute-start(f16[56,1024]{1,0:T(8,128)(2,1)S(1)} %get-tuple-element.20), channel_id=1, source_target_pairs={{0,2},{1,3},{2,0},{3,1},{4,6},{5,7},{6,4},{7,5},{8,10},{9,11},{10,... | collective-permute-start | bytes 344072 | tf_op jit(solution)/shard_map/ppermute | solution.py:24
  57.1 7.1 %collective-permute-start.17 = (f16[56,1024]{1,0:T(8,128)(2,1)S(1)}, f16[56,1024]{1,0:T(8,128)(2,1)S(1)}, u32[]{:S(2)}, u32[]{:S(2)}) collective-permute-start(f16[56,1024]{1,0:T(8,128)(2,1)S(1)} %get-tuple-element.21), channel_id=1, source_target_pairs={{0,6},{1,7},{2,4},{3,5},{4,2},{5,3},{6,0},{7,1},{8,14},{9,15},{10,... | collective-permute-start | bytes 344072 | tf_op jit(solution)/shard_map/ppermute | solution.py:24
  58.5 7.1 %collective-permute-start.16 = (f16[56,1024]{1,0:T(8,128)(2,1)S(1)}, f16[56,1024]{1,0:T(8,128)(2,1)S(1)}, u32[]{:S(2)}, u32[]{:S(2)}) collective-permute-start(f16[56,1024]{1,0:T(8,128)(2,1)S(1)} %get-tuple-element.22), channel_id=1, source_target_pairs={{0,4},{1,5},{2,6},{3,7},{4,0},{5,1},{6,2},{7,3},{8,12},{9,13},{10,... | collective-permute-start | bytes 344072 | tf_op jit(solution)/shard_map/ppermute | solution.py:24
  65.7 7.9 %collective-permute-start.20 = (f16[56,1024]{1,0:T(8,128)(2,1)S(1)}, f16[56,1024]{1,0:T(8,128)(2,1)S(1)}, u32[]{:S(2)}, u32[]{:S(2)}) collective-permute-start(f16[56,1024]{1,0:T(8,128)(2,1)S(1)} %fusion.19), channel_id=1, source_target_pairs={{0,24},{1,25},{2,26},{3,27},{4,28},{5,29},{6,30},{7,31},{8,16},{9,... | collective-permute-start | bytes 344072 | tf_op jit(solution)/shard_map/ppermute | solution.py:24
  67.2 9.7 %collective-permute-start.19 = (f16[56,1024]{1,0:T(8,128)(2,1)S(1)}, f16[56,1024]{1,0:T(8,128)(2,1)S(1)}, u32[]{:S(2)}, u32[]{:S(2)}) collective-permute-start(f16[56,1024]{1,0:T(8,128)(2,1)S(1)} %fusion.19), channel_id=1, source_target_pairs={{0,16},{1,17},{2,18},{3,19},{4,20},{5,21},{6,22},{7,23},{8,24},{9,... | collective-permute-start | bytes 344072 | tf_op jit(solution)/shard_map/ppermute | solution.py:24
  67.2 9.7 %collective-permute-start.18 = (f16[56,1024]{1,0:T(8,128)(2,1)S(1)}, f16[56,1024]{1,0:T(8,128)(2,1)S(1)}, u32[]{:S(2)}, u32[]{:S(2)}) collective-permute-start(f16[56,1024]{1,0:T(8,128)(2,1)S(1)} %fusion.19), channel_id=1, source_target_pairs={{0,8},{1,9},{2,10},{3,11},{4,12},{5,13},{6,14},{7,15},{8,0},{9,1},... | collective-permute-start | bytes 344072 | tf_op jit(solution)/shard_map/ppermute | solution.py:24
  77.1 6.9 %collective-permute-start.23 = (bf16[56,1024]{1,0:T(8,128)(2,1)S(1)}, bf16[56,1024]{1,0:T(8,128)(2,1)S(1)}, u32[]{:S(2)}, u32[]{:S(2)}) collective-permute-start(bf16[56,1024]{1,0:T(8,128)(2,1)S(1)} %multiply_convert_fusion), channel_id=1, source_target_pairs={{0,6},{1,7},{2,4},{3,5},{4,2},{5,3},{6,0},{7,1},{8,14},{9,15},{10,... | collective-permute-start | bytes 344072 | tf_op jit(solution)/shard_map/ppermute | solution.py:24
  78.7 6.9 %collective-permute-start.22 = (bf16[56,1024]{1,0:T(8,128)(2,1)S(1)}, bf16[56,1024]{1,0:T(8,128)(2,1)S(1)}, u32[]{:S(2)}, u32[]{:S(2)}) collective-permute-start(bf16[56,1024]{1,0:T(8,128)(2,1)S(1)} %multiply_convert_fusion), channel_id=1, source_target_pairs={{0,4},{1,5},{2,6},{3,7},{4,0},{5,1},{6,2},{7,3},{8,12},{9,13},{10,... | collective-permute-start | bytes 344072 | tf_op jit(solution)/shard_map/ppermute | solution.py:24
  80.0 5.6 %collective-permute-start.21 = (bf16[56,1024]{1,0:T(8,128)(2,1)S(1)}, bf16[56,1024]{1,0:T(8,128)(2,1)S(1)}, u32[]{:S(2)}, u32[]{:S(2)}) collective-permute-start(bf16[56,1024]{1,0:T(8,128)(2,1)S(1)} %multiply_convert_fusion), channel_id=1, source_target_pairs={{0,2},{1,3},{2,0},{3,1},{4,6},{5,7},{6,4},{7,5},{8,10},{9,11},{10,... | collective-permute-start | bytes 344072 | tf_op jit(solution)/shard_map/ppermute | solution.py:24
  85.7 1.9 %collective-permute-start.24 = (bf16[224,1024]{1,0:T(8,128)(2,1)S(1)}, bf16[224,1024]{1,0:T(8,128)(2,1)S(1)}, u32[]{:S(2)}, u32[]{:S(2)}) collective-permute-start(bf16[224,1024]{1,0:T(8,128)(2,1)S(1)} %pad_maximum_fusion.1.mine_ref), channel_id=1, source_target_pairs={{0,1},{1,0},{2,3},{3,2},{4,5},{5,4},{6,7},{7,6},{8,9},{9,8},{10,11... | collective-permute-start | bytes 1376264 | tf_op jit(solution)/shard_map/ppermute | solution.py:24

commit v3 on v2

--- a/solution.py
+++ b/solution.py
@@ -40,6 +40,95 @@
     return encode, decode
 
 
+EXTRA = 2
+PER_WORD = 16 // EXTRA
+PIECES = 3
+LOWEST = -28
+SHIFT = 15 + EXTRA
+LANES = 128
+
+
+def power_of_two(number, sign):
+    power = jnp.ones(number.shape, jnp.float32)
+    for bit in range(6):
+        power = power * jnp.where((number >> bit) & 1 == 1, 2.0 ** (sign * (1 << bit)), 1.0)
+    return power
+
+
+def words_for(tiles):
+    return -(-(tiles + 1) // PER_WORD)
+
+
+def encode_fixed(value, out_ref):
+    rows, width = value.shape
+    tiles = rows // ROW_TILE
+    largest = jnp.max(jnp.abs(value), axis=1, keepdims=True)
+    exponent = jnp.ceil(jnp.log2(jnp.maximum(largest, 2.0 ** LOWEST) * 1.001))
+    exponent = jnp.clip(exponent.astype(jnp.int32) - LOWEST, 0, 63)
+    inverse = power_of_two(exponent, -1) * 2.0 ** (SHIFT - LOWEST)
+    whole = jnp.clip(jnp.round(value * inverse), -(2.0 ** SHIFT), 2.0 ** SHIFT - 1.0)
+    number = whole.astype(jnp.int32)
+    lower = number & ((1 << EXTRA) - 1)
+    lane = lax.broadcasted_iota(jnp.int32, (ROW_TILE, width), 1)
+    marked = jnp.zeros((ROW_TILE, width), jnp.int32)
+    for t in range(tiles):
+        scale = exponent[t * ROW_TILE:(t + 1) * ROW_TILE]
+        for i in range(PIECES):
+            piece = (scale >> (EXTRA * i)) & ((1 << EXTRA) - 1)
+            marked = jnp.where(lane == PIECES * t + i, piece, marked)
+    slots = [lower[t * ROW_TILE:(t + 1) * ROW_TILE] for t in range(tiles)] + [marked]
+    packed = []
+    for w in range(words_for(tiles)):
+        word = jnp.full((ROW_TILE, width), -(1 << 15), jnp.int32)
+        for i, slot in enumerate(slots[w * PER_WORD:(w + 1) * PER_WORD]):
+            word = word + (slot << (EXTRA * i))
+        packed.append(word)
+    out_ref[...] = jnp.concatenate([number >> EXTRA] + packed, axis=0).astype(jnp.int16)
+    return whole * (power_of_two(exponent, 1) * 2.0 ** (LOWEST - SHIFT))
+
+
+def decode_fixed(ref, rows):
+    tiles = rows // ROW_TILE
+    sent = ref[...].astype(jnp.int32)
+    packed = [
+        sent[rows + w * ROW_TILE:rows + (w + 1) * ROW_TILE] + (1 << 15) for w in range(words_for(tiles))
+    ]
+    slots = [(packed[t // PER_WORD] >> (EXTRA * (t % PER_WORD))) & ((1 << EXTRA) - 1) for t in range(tiles + 1)]
+    number = (sent[:rows] << EXTRA) + jnp.concatenate(slots[:tiles], axis=0)
+    marked = slots[tiles][:, :LANES].astype(jnp.float32)
+    lane = lax.broadcasted_iota(jnp.int32, (ROW_TILE, LANES), 1)
+    exponents = []
+    for t in range(tiles):
+        scale = jnp.zeros((ROW_TILE, LANES), jnp.float32)
+        for i in range(PIECES):
+            scale = jnp.where(lane == PIECES * t + i, marked * float(1 << (EXTRA * i)), scale)
+        exponents.append(jnp.sum(scale, axis=1, keepdims=True))
+    exponent = jnp.concatenate(exponents, axis=0).astype(jnp.int32)
+    unit = power_of_two(exponent, 1) * 2.0 ** (LOWEST - SHIFT)
+    return number.astype(jnp.float32) * unit
+
+
+def encode_kernel(kept_ref, received_ref, own_ref, *out_refs):
+    rows = own_ref.shape[0]
+    own_ref[...] = kept_ref[pl.ds(0, rows), :] + received_ref[pl.ds(0, rows), :]
+    for k, out_ref in enumerate(out_refs):
+        span = pl.ds((k + 1) * rows, rows)
+        encode_fixed(kept_ref[span, :] + received_ref[span, :], out_ref)
+
+
+def sum_received(own_ref, refs):
+    return four_sum(own_ref[...], [decode_fixed(ref, own_ref.shape[0]) for ref in refs])
+
+
+def recode_kernel(own_ref, *refs):
+    refs, (total_ref, out_ref) = refs[:-2], refs[-2:]
+    total_ref[...] = encode_fixed(sum_received(own_ref, refs), out_ref)
+
+
+def finish_kernel(own_ref, *refs):
+    refs[-1][...] = normalise(sum_received(own_ref, refs[:-1]))
+
+
 def normalise(total):
     scale = lax.rsqrt(jnp.mean(total * total, axis=1, keepdims=True) + epsilon)
     return (total * scale).astype(jnp.bfloat16)
@@ -55,16 +144,17 @@
     return [swap(sent, devices, bit * k) for k in steps]
 
 
-def in_plane(kept, given, devices, encode, decode):
+def across_cores(kept, given, devices):
+    return lax.optimization_barrier((kept, swap(given, devices, 1)))
+
+
+def half_block(kept, given, devices, bound):
+    kept, received = across_cores(kept, given, devices)
+    chip = kept + received
     rows = kept.shape[0] // 4
-    kept, received = lax.optimization_barrier((kept, swap(given, devices, 1)))
-    chip = kept + received
+    encode, decode = to_half(2.0 * bound)
     others = [decode(swap(encode(chip[k * rows:(k + 1) * rows]), devices, 2 * k)) for k in range(1, 4)]
-    return four_sum(chip[:rows], others)
-
-
-def half_block(kept, given, devices, bound):
-    total = in_plane(kept, given, devices, *to_half(2.0 * bound))
+    total = four_sum(chip[:rows], others)
     bound = 8.0 * bound
     bit = 8
     while bit < devices:
@@ -77,34 +167,29 @@
     return normalise(total)
 
 
-def full_block(kept, given, devices, used):
-    total = in_plane(kept, given, devices, lambda value: value, lambda value: value)
-    rows, samples = total.shape
+def full_block(kept, given, devices):
+    kept, received = across_cores(kept, given, devices)
+    rows, samples = kept.shape[0] // 4, kept.shape[1]
+    own = pltpu.VMEM((rows, samples), jnp.float32)
+    coded = pltpu.VMEM((rows + ROW_TILE * words_for(rows // ROW_TILE), samples), jnp.int16)
+
+    def call(kernel, out_shape, *operands):
+        return pl.pallas_call(
+            kernel,
+            out_shape=out_shape,
+            in_specs=in_vmem(len(operands)),
+            out_specs=in_vmem(len(out_shape)),
+            compiler_params=pltpu.CompilerParams(vmem_limit_bytes=KERNEL_BYTES),
+        )(*[on_chip(operand) for operand in operands])
+
+    total, *sent = call(encode_kernel, [own] + [coded] * 3, kept, received)
+    others = [swap(sent[k - 1], devices, 2 * k) for k in range(1, 4)]
     bit = 8
-    members = min(4, devices // bit)
-    if members < 2:
-        return normalise(total)
-    part = -(-used // members)
-    member = (lax.axis_index(AXIS) // bit) % members
-    lanes = 128
-    parts = jnp.pad(total, ((0, max(0, part * members - rows)), (0, 0)))[:part * members]
-    parts = parts.reshape(members, part, samples // lanes, lanes)
-
-    def part_of(k):
-        return lax.dynamic_index_in_dim(parts, member ^ k, 0, keepdims=False)
-
-    total = four_sum(part_of(0), [swap(part_of(k), devices, bit * k) for k in range(1, members)])
-    rest = bit * members
-    while rest < devices:
-        others = spread(total, devices, rest)
-        total = four_sum(total, others)
-        rest = rest * (len(others) + 1)
-    scale = lax.rsqrt(jnp.sum(total * total, axis=(1, 2), keepdims=True) * (1.0 / samples) + epsilon)
-    mine = (total * scale).astype(jnp.bfloat16)
-    pieces = jnp.stack([mine] + spread(mine, devices, bit))
-    ordered = [lax.dynamic_index_in_dim(pieces, member ^ m, 0, keepdims=False) for m in range(members)]
-    block = jnp.concatenate(ordered, axis=0)[:rows].reshape(-1, samples)
-    return jnp.pad(block, ((0, rows - block.shape[0]), (0, 0)))
+    while bit < devices:
+        total, sent = call(recode_kernel, [own, coded], total, *others)
+        others = spread(sent, devices, bit)
+        bit = bit * (len(others) + 1)
+    return call(finish_kernel, [pltpu.VMEM((rows, samples), jnp.bfloat16)], total, *others)[0]
 
 
 def gather_blocks(block, devices):
@@ -132,15 +217,18 @@
     return (block ^ mine) * rows + (label - block * used)
 
 
-def first_kernel(mine_ref, label_ref, expression_ref, standard_ref, given_ref, buffer, sems):
+def first_kernel(mine_ref, label_hbm, expression_ref, standard_ref, given_ref, buffer, label_ref, sems, label_sem):
     genes, samples = standard_ref.shape
     size = genes // CHUNKS
     copies = [
         pltpu.make_async_copy(expression_ref.at[pl.ds(c * size, size)], buffer.at[pl.ds(c * size, size)], sems.at[c])
         for c in range(CHUNKS)
     ]
+    label_copy = pltpu.make_async_copy(label_hbm, label_ref, label_sem)
+    label_copy.start()
     for copy in copies:
         copy.start()
+    label_copy.wait()
     slot = slots(label_ref[...], mine_ref[0], given_ref.shape[0] // (BLOCKS // 2)) - given_ref.shape[0]
     for c, copy in enumerate(copies):
         copy.wait()
@@ -219,20 +307,25 @@
             out_shape=[pltpu.VMEM((genes, samples), jnp.bfloat16), pltpu.VMEM((half, samples), f32)],
             in_specs=[
                 pl.BlockSpec(memory_space=pltpu.SMEM),
-                pl.BlockSpec(memory_space=pltpu.VMEM),
+                pl.BlockSpec(memory_space=pltpu.HBM),
                 pl.BlockSpec(memory_space=pltpu.HBM),
             ],
             out_specs=in_vmem(2),
-            scratch_shapes=[pltpu.VMEM((genes, samples), jnp.bfloat16), pltpu.SemaphoreType.DMA((CHUNKS,))],
+            scratch_shapes=[
+                pltpu.VMEM((genes, samples), jnp.bfloat16),
+                pltpu.VMEM((1, genes), jnp.int32),
+                pltpu.SemaphoreType.DMA((CHUNKS,)),
+                pltpu.SemaphoreType.DMA,
+            ],
             name="first",
                 compiler_params=pltpu.CompilerParams(vmem_limit_bytes=KERNEL_BYTES),
-        )(mine[None], labels[None, :], pltpu.with_memory_space_constraint(expression, pltpu.HBM))
+        )(mine[None], pltpu.with_memory_space_constraint(labels[None, :], pltpu.HBM), pltpu.with_memory_space_constraint(expression, pltpu.HBM))
         slot = slots(labels, mine, rows)
         column = jnp.arange(half, dtype=jnp.int32)
         kept = weigh((slot[:, None] == column[None, :]).astype(jnp.bfloat16), standard)
         for iteration in range(ITERS):
             last = iteration == ITERS - 1
-            block = half_block(kept, given, devices, bound) if last else full_block(kept, given, devices, used)
+            block = half_block(kept, given, devices, bound) if last else full_block(kept, given, devices)
             own, other = gather_blocks(block, devices)
             if not last:
                 mine_raised = raise_half(own, standard, 0, mine)

time: 91.3 us -> 82.6 us (0.905)
  starting transfers between devices: 29.2 us -> 24.9 us
  waiting for transfers between devices: 47.2 us -> 43.6 us
  Pallas kernels: 6.52 us -> 8.29 us
  other arithmetic: 2.34 us -> 0.78 us
    ppermute x25 -> x22, starting transfers between devices: 29.2 us -> 24.9 us  [swap(): return lax.ppermute(value, AXIS, [(i, i ^ bit) for i in range(devices)])]
    ppermute x25 -> x22, waiting for transfers between devices: 47.2 us -> 43.6 us  [swap(): return lax.ppermute(value, AXIS, [(i, i ^ bit) for i in range(devices)])]
    pallas_call x0 -> x3, Pallas kernels: none -> 1.51 us  [call(): pl.pallas_call(kernel, out_shape=out_shape, in_specs=in_vmem(len(operands...]
    add x3 -> x1, other arithmetic: 1.26 us -> 0.14 us  [half_block(): chip = kept + received]
  transfers between devices with their start and end apart: 25 -> 22, of which waited for: 22 -> 18; matrix products, arithmetic and copies ran while one was open for 3% -> 3% of each run, Pallas kernels for 0% -> 0%
where the time goes in v3:
time: 82.6 us; the launch traced here: 82.5 us
  waiting for transfers between devices  43.6 us (53%)
  starting transfers between devices  24.9 us (30%)
  Pallas kernels  8.29 us (10%)
  matrix products  4.02 us (5%)
    ppermute x22, waiting for transfers between devices, swap(): return lax.ppermute(value, AXIS, [(i, i ^ bit) for i in range(devices)])  43.6 us
    ppermute x22, starting transfers between devices, swap(): return lax.ppermute(value, AXIS, [(i, i ^ bit) for i in range(devices)])  24.9 us
    pallas_call x1, Pallas kernels, body(): pl.pallas_call(last_kernel, out_shape=[jax.ShapeDtypeStruct((MODULES, gen...  3.55 us
    pallas_call x1, Pallas kernels, body(): pl.pallas_call(first_kernel, out_shape=[pltpu.VMEM((genes, samples), jnp....  3.23 us
    dot_general x3, matrix products, weigh(): lax.dot_general(weights, standard, (((0,), (0,)), ((), ())), preferred_el...  2.26 us
    dot_general x2, matrix products, dot_tt(): lax.dot_general(a, b, (((1,), (1,)), ((), ())), preferred_element_type=jn...  1.76 us
  transfers between devices with their start and end apart: 22, of which 18 were waited for; matrix products, arithmetic and copies ran while one was open for 3% of the time, Pallas kernels for 0%

profile of v3, /device:TPU:0, one launch (start us, length us, event | category | flops | bytes accessed | tf_op | source)
XLA Modules:
  0.0 82.5 jit_solution(9727590399843517978)
XLA Ops:
  0.6 0.0 copy-start
  0.6 3.2 %first.1 = (bf16[1024,1024]{1,0:T(8,128)(2,1)S(1)}, f32[224,1024]{1,0:T(8,128)S(1)}) custom-call(s32[1]{0:T(128)} %bitcast.mine_ref, s32[1,1024]{1,0:T(1,128)} %bitcast.9, bf16[1024,1024]{1,0:T(8,128)(2,1)} %expression_ref.1), custom_call_target="tpu_custom_call" | custom-call | tf_op jit(solution)/shard_map/first/pallas_call | solution.py:305
  3.9 0.6 collective-permute-start
  4.4 0.0 copy-done
  4.5 1.0 %fusion.4.kept_ref = f32[224,1024]{1,0:T(8,128)S(1)} fusion(bf16[1024,1024]{1,0:T(8,128)(2,1)S(1)} %get-tuple-element.16.standard_ref, s32[1024]{0:T(1024)S(1)} %subtract_add_fusion), kind=kOutput, calls=%fused_computation.7 | convolution fusion | flops 469991424 | bytes 3018752 | tf_op jit(solution)/shard_map/dot_general | solution.py:262
  5.4 1.1 %collective-permute-done.received_ref = f32[224,1024]{1,0:T(8,128)S(1)} collective-permute-done((f32[224,1024]{1,0:T(8,128)S(1)}, f32[224,1024]{1,0:T(8,128)S(1)}, u32[]{:S(2)}, u32[]{:S(2)}) %collective-permute-start) | collective-permute-done | bytes 917536 | tf_op jit(solution)/shard_map/ppermute | solution.py:24
  6.5 0.5 shard_map.41
  7.0 2.9 %collective-permute-start.1 = (s16[64,1024]{1,0:T(8,128)(2,1)S(1)}, s16[64,1024]{1,0:T(8,128)(2,1)S(1)}, u32[]{:S(2)}, u32[]{:S(2)}) collective-permute-start(s16[64,1024]{1,0:T(8,128)(2,1)S(1)} %get-tuple-element.21), channel_id=1, source_target_pairs={{0,2},{1,3},{2,0},{3,1},{4,6},{5,7},{6,4},{7,5},{8,10},{9,11},{10,... | collective-permute-start | bytes 393224 | tf_op jit(solution)/shard_map/ppermute | solution.py:24
  9.9 1.5 %collective-permute-start.2 = (s16[64,1024]{1,0:T(8,128)(2,1)S(1)}, s16[64,1024]{1,0:T(8,128)(2,1)S(1)}, u32[]{:S(2)}, u32[]{:S(2)}) collective-permute-start(s16[64,1024]{1,0:T(8,128)(2,1)S(1)} %get-tuple-element.22), channel_id=1, source_target_pairs={{0,4},{1,5},{2,6},{3,7},{4,0},{5,1},{6,2},{7,3},{8,12},{9,13},{10,... | collective-permute-start | bytes 393224 | tf_op jit(solution)/shard_map/ppermute | solution.py:24
  11.5 0.0 collective-permute-start.3
  11.5 2.4 %collective-permute-done.1.refs_0_ = s16[64,1024]{1,0:T(8,128)(2,1)S(1)} collective-permute-done((s16[64,1024]{1,0:T(8,128)(2,1)S(1)}, s16[64,1024]{1,0:T(8,128)(2,1)S(1)}, u32[]{:S(2)}, u32[]{:S(2)}) %collective-permute-start.1) | collective-permute-done | bytes 131104 | tf_op jit(solution)/shard_map/ppermute | solution.py:24
  13.9 4.1 %collective-permute-done.2.refs_1_ = s16[64,1024]{1,0:T(8,128)(2,1)S(1)} collective-permute-done((s16[64,1024]{1,0:T(8,128)(2,1)S(1)}, s16[64,1024]{1,0:T(8,128)(2,1)S(1)}, u32[]{:S(2)}, u32[]{:S(2)}) %collective-permute-start.2) | collective-permute-done | bytes 131104 | tf_op jit(solution)/shard_map/ppermute | solution.py:24
  18.0 0.0 collective-permute-done.3.refs_2_
  18.0 0.6 shard_map.42
  18.6 3.7 %collective-permute-start.6 = (s16[64,1024]{1,0:T(8,128)(2,1)S(1)}, s16[64,1024]{1,0:T(8,128)(2,1)S(1)}, u32[]{:S(2)}, u32[]{:S(2)}) collective-permute-start(s16[64,1024]{1,0:T(8,128)(2,1)S(1)} %get-tuple-element.25), channel_id=1, source_target_pairs={{0,24},{1,25},{2,26},{3,27},{4,28},{5,29},{6,30},{7,31},{8,16},{9,... | collective-permute-start | bytes 393224 | tf_op jit(solution)/shard_map/ppermute | solution.py:24
  22.3 0.0 collective-permute-start.5
  22.3 0.8 collective-permute-start.4
  23.0 3.8 %collective-permute-done.6.refs_2_ = s16[64,1024]{1,0:T(8,128)(2,1)S(1)} collective-permute-done((s16[64,1024]{1,0:T(8,128)(2,1)S(1)}, s16[64,1024]{1,0:T(8,128)(2,1)S(1)}, u32[]{:S(2)}, u32[]{:S(2)}) %collective-permute-start.6) | collective-permute-done | bytes 131104 | tf_op jit(solution)/shard_map/ppermute | solution.py:24
  26.8 5.6 %collective-permute-done.5.refs_1_ = s16[64,1024]{1,0:T(8,128)(2,1)S(1)} collective-permute-done((s16[64,1024]{1,0:T(8,128)(2,1)S(1)}, s16[64,1024]{1,0:T(8,128)(2,1)S(1)}, u32[]{:S(2)}, u32[]{:S(2)}) %collective-permute-start.5) | collective-permute-done | bytes 131104 | tf_op jit(solution)/shard_map/ppermute | solution.py:24
  32.4 0.0 collective-permute-done.4.refs_0_
  32.4 0.5 shard_map.43
  32.9 1.6 %collective-permute-start.9 = (bf16[56,1024]{1,0:T(8,128)(2,1)S(1)}, bf16[56,1024]{1,0:T(8,128)(2,1)S(1)}, u32[]{:S(2)}, u32[]{:S(2)}) collective-permute-start(bf16[56,1024]{1,0:T(8,128)(2,1)S(1)} %shard_map.43), channel_id=1, source_target_pairs={{0,6},{1,7},{2,4},{3,5},{4,2},{5,3},{6,0},{7,1},{8,14},{9,15},{10,... | collective-permute-start | bytes 344072 | tf_op jit(solution)/shard_map/ppermute | solution.py:24
  34.5 1.5 %collective-permute-start.8 = (bf16[56,1024]{1,0:T(8,128)(2,1)S(1)}, bf16[56,1024]{1,0:T(8,128)(2,1)S(1)}, u32[]{:S(2)}, u32[]{:S(2)}) collective-permute-start(bf16[56,1024]{1,0:T(8,128)(2,1)S(1)} %shard_map.43), channel_id=1, source_target_pairs={{0,4},{1,5},{2,6},{3,7},{4,0},{5,1},{6,2},{7,3},{8,12},{9,13},{10,... | collective-permute-start | bytes 344072 | tf_op jit(solution)/shard_map/ppermute | solution.py:24
  36.0 0.4 collective-permute-start.7
  36.4 3.3 %collective-permute-done.9 = bf16[56,1024]{1,0:T(8,128)(2,1)S(1)} collective-permute-done((bf16[56,1024]{1,0:T(8,128)(2,1)S(1)}, bf16[56,1024]{1,0:T(8,128)(2,1)S(1)}, u32[]{:S(2)}, u32[]{:S(2)}) %collective-permute-start.9) | collective-permute-done | bytes 114720 | tf_op jit(solution)/shard_map/ppermute | solution.py:24
  39.8 0.8 collective-permute-done.8
  40.5 0.4 collective-permute-done.7
  40.9 0.1 collective-permute-start.10
  41.1 0.9 %fusion.27 = (f32[1024]{0:T(1024)S(1)}, f32[1024,224]{0,1:T(8,128)S(1)}) fusion(bf16[1024,1024]{1,0:T(8,128)(2,1)S(1)} %get-tuple-element.16.standard_ref, bf16[56,1024]{1,0:T(8,128)(2,1)S(1)} %collective-permute-done.9, bf16[56,1024]{1,0:T(8,128)(2,1)S(1)} %collective-permute-done.8, bf16[56,1024]{1,0:T(8,128)(2,1)S(1)} %collective-permute-done.7, ...), kind=kOutput, calls=%fused_computation.55 | convolution fusion | flops 472284160 | bytes 3477728 | tf_op jit(solution)/shard_map/dot_general | solution.py:205
  41.9 0.9 %collective-permute-done.10 = bf16[224,1024]{1,0:T(8,128)(2,1)S(1)} collective-permute-done((bf16[224,1024]{1,0:T(8,128)(2,1)S(1)}, bf16[224,1024]{1,0:T(8,128)(2,1)S(1)}, u32[]{:S(2)}, u32[]{:S(2)}) %collective-permute-start.10) | collective-permute-done | bytes 458784 | tf_op jit(solution)/shard_map/ppermute | solution.py:24
  42.8 0.9 %fusion.28 = (f32[1024]{0:T(1024)S(1)}, f32[1024,224]{0,1:T(8,128)S(1)}) fusion(bf16[1024,1024]{1,0:T(8,128)(2,1)S(1)} %get-tuple-element.16.standard_ref, bf16[224,1024]{1,0:T(8,128)(2,1)S(1)} %collective-permute-done.10, pred[224]{0:T(512)(128)(4,1)S(1)} %compare_and_fusion), kind=kOutput, calls=%fused_computation.56 | convolution fusion | flops 470449152 | bytes 3477728 | tf_op jit(solution)/shard_map/dot_general | solution.py:205
  43.7 0.6 fusion.7
  44.4 0.2 collective-permute-start.11
  44.6 0.7 fusion.6
  45.2 1.7 %collective-permute-done.11 = f32[224,1024]{1,0:T(8,128)S(1)} collective-permute-done((f32[224,1024]{1,0:T(8,128)S(1)}, f32[224,1024]{1,0:T(8,128)S(1)}, u32[]{:S(2)}, u32[]{:S(2)}) %collective-permute-start.11) | collective-permute-done | bytes 917536 | tf_op jit(solution)/shard_map/ppermute | solution.py:24
  46.9 0.1 add.170
  47.0 0.1 fusion.16
  47.1 1.3 %collective-permute-start.12 = (f16[56,1024]{1,0:T(8,128)(2,1)S(1)}, f16[56,1024]{1,0:T(8,128)(2,1)S(1)}, u32[]{:S(2)}, u32[]{:S(2)}) collective-permute-start(f16[56,1024]{1,0:T(8,128)(2,1)S(1)} %get-tuple-element.30), channel_id=1, source_target_pairs={{0,2},{1,3},{2,0},{3,1},{4,6},{5,7},{6,4},{7,5},{8,10},{9,11},{10,... | collective-permute-start | bytes 344072 | tf_op jit(solution)/shard_map/ppermute | solution.py:24
  48.4 1.4 %collective-permute-start.14 = (f16[56,1024]{1,0:T(8,128)(2,1)S(1)}, f16[56,1024]{1,0:T(8,128)(2,1)S(1)}, u32[]{:S(2)}, u32[]{:S(2)}) collective-permute-start(f16[56,1024]{1,0:T(8,128)(2,1)S(1)} %get-tuple-element.31), channel_id=1, source_target_pairs={{0,6},{1,7},{2,4},{3,5},{4,2},{5,3},{6,0},{7,1},{8,14},{9,15},{10,... | collective-permute-start | bytes 344072 | tf_op jit(solution)/shard_map/ppermute | solution.py:24
  49.9 0.8 collective-permute-start.13
  50.7 2.5 %collective-permute-done.12 = f16[56,1024]{1,0:T(8,128)(2,1)S(1)} collective-permute-done((f16[56,1024]{1,0:T(8,128)(2,1)S(1)}, f16[56,1024]{1,0:T(8,128)(2,1)S(1)}, u32[]{:S(2)}, u32[]{:S(2)}) %collective-permute-start.12) | collective-permute-done | bytes 114720 | tf_op jit(solution)/shard_map/ppermute | solution.py:24
  53.2 2.4 %collective-permute-done.14 = f16[56,1024]{1,0:T(8,128)(2,1)S(1)} collective-permute-done((f16[56,1024]{1,0:T(8,128)(2,1)S(1)}, f16[56,1024]{1,0:T(8,128)(2,1)S(1)}, u32[]{:S(2)}, u32[]{:S(2)}) %collective-permute-start.14) | collective-permute-done | bytes 114720 | tf_op jit(solution)/shard_map/ppermute | solution.py:24
  55.6 1.4 %collective-permute-done.13 = f16[56,1024]{1,0:T(8,128)(2,1)S(1)} collective-permute-done((f16[56,1024]{1,0:T(8,128)(2,1)S(1)}, f16[56,1024]{1,0:T(8,128)(2,1)S(1)}, u32[]{:S(2)}, u32[]{:S(2)}) %collective-permute-start.13) | collective-permute-done | bytes 114720 | tf_op jit(solution)/shard_map/ppermute | solution.py:24
  57.0 0.1 fusion.19
  57.1 1.9 %collective-permute-start.17 = (f16[56,1024]{1,0:T(8,128)(2,1)S(1)}, f16[56,1024]{1,0:T(8,128)(2,1)S(1)}, u32[]{:S(2)}, u32[]{:S(2)}) collective-permute-start(f16[56,1024]{1,0:T(8,128)(2,1)S(1)} %fusion.19), channel_id=1, source_target_pairs={{0,24},{1,25},{2,26},{3,27},{4,28},{5,29},{6,30},{7,31},{8,16},{9,... | collective-permute-start | bytes 344072 | tf_op jit(solution)/shard_map/ppermute | solution.py:24
  58.9 0.0 collective-permute-start.16
  59.0 2.6 %collective-permute-start.15 = (f16[56,1024]{1,0:T(8,128)(2,1)S(1)}, f16[56,1024]{1,0:T(8,128)(2,1)S(1)}, u32[]{:S(2)}, u32[]{:S(2)}) collective-permute-start(f16[56,1024]{1,0:T(8,128)(2,1)S(1)} %fusion.19), channel_id=1, source_target_pairs={{0,8},{1,9},{2,10},{3,11},{4,12},{5,13},{6,14},{7,15},{8,0},{9,1},... | collective-permute-start | bytes 344072 | tf_op jit(solution)/shard_map/ppermute | solution.py:24
  61.5 3.5 %collective-permute-done.17 = f16[56,1024]{1,0:T(8,128)(2,1)S(1)} collective-permute-done((f16[56,1024]{1,0:T(8,128)(2,1)S(1)}, f16[56,1024]{1,0:T(8,128)(2,1)S(1)}, u32[]{:S(2)}, u32[]{:S(2)}) %collective-permute-start.17) | collective-permute-done | bytes 114720 | tf_op jit(solution)/shard_map/ppermute | solution.py:24
  65.0 3.2 %collective-permute-done.16 = f16[56,1024]{1,0:T(8,128)(2,1)S(1)} collective-permute-done((f16[56,1024]{1,0:T(8,128)(2,1)S(1)}, f16[56,1024]{1,0:T(8,128)(2,1)S(1)}, u32[]{:S(2)}, u32[]{:S(2)}) %collective-permute-start.16) | collective-permute-done | bytes 114720 | tf_op jit(solution)/shard_map/ppermute | solution.py:24
  68.2 0.0 collective-permute-done.15
  68.2 0.2 multiply_reduce_fusion
  68.4 0.1 multiply_convert_fusion
  68.5 1.5 %collective-permute-start.20 = (bf16[56,1024]{1,0:T(8,128)(2,1)S(1)}, bf16[56,1024]{1,0:T(8,128)(2,1)S(1)}, u32[]{:S(2)}, u32[]{:S(2)}) collective-permute-start(bf16[56,1024]{1,0:T(8,128)(2,1)S(1)} %multiply_convert_fusion), channel_id=1, source_target_pairs={{0,6},{1,7},{2,4},{3,5},{4,2},{5,3},{6,0},{7,1},{8,14},{9,15},{10,... | collective-permute-start | bytes 344072 | tf_op jit(solution)/shard_map/ppermute | solution.py:24
  70.0 1.0 %collective-permute-start.19 = (bf16[56,1024]{1,0:T(8,128)(2,1)S(1)}, bf16[56,1024]{1,0:T(8,128)(2,1)S(1)}, u32[]{:S(2)}, u32[]{:S(2)}) collective-permute-start(bf16[56,1024]{1,0:T(8,128)(2,1)S(1)} %multiply_convert_fusion), channel_id=1, source_target_pairs={{0,4},{1,5},{2,6},{3,7},{4,0},{5,1},{6,2},{7,3},{8,12},{9,13},{10,... | collective-permute-start | bytes 344072 | tf_op jit(solution)/shard_map/ppermute | solution.py:24
  71.1 1.0 %collective-permute-start.18 = (bf16[56,1024]{1,0:T(8,128)(2,1)S(1)}, bf16[56,1024]{1,0:T(8,128)(2,1)S(1)}, u32[]{:S(2)}, u32[]{:S(2)}) collective-permute-start(bf16[56,1024]{1,0:T(8,128)(2,1)S(1)} %multiply_convert_fusion), channel_id=1, source_target_pairs={{0,2},{1,3},{2,0},{3,1},{4,6},{5,7},{6,4},{7,5},{8,10},{9,11},{10,... | collective-permute-start | bytes 344072 | tf_op jit(solution)/shard_map/ppermute | solution.py:24
  72.1 3.4 %collective-permute-done.20 = bf16[56,1024]{1,0:T(8,128)(2,1)S(1)} collective-permute-done((bf16[56,1024]{1,0:T(8,128)(2,1)S(1)}, bf16[56,1024]{1,0:T(8,128)(2,1)S(1)}, u32[]{:S(2)}, u32[]{:S(2)}) %collective-permute-start.20) | collective-permute-done | bytes 114720 | tf_op jit(solution)/shard_map/ppermute | solution.py:24
  75.5 1.5 %collective-permute-done.19 = bf16[56,1024]{1,0:T(8,128)(2,1)S(1)} collective-permute-done((bf16[56,1024]{1,0:T(8,128)(2,1)S(1)}, bf16[56,1024]{1,0:T(8,128)(2,1)S(1)}, u32[]{:S(2)}, u32[]{:S(2)}) %collective-permute-start.19) | collective-permute-done | bytes 114720 | tf_op jit(solution)/shard_map/ppermute | solution.py:24
  77.0 0.0 collective-permute-done.18
  77.0 0.1 collective-permute-start.21
  77.1 0.1 fusion.24.source_ref
  77.2 1.7 %collective-permute-done.21.other_ref = bf16[224,1024]{1,0:T(8,128)(2,1)S(1)} collective-permute-done((bf16[224,1024]{1,0:T(8,128)(2,1)S(1)}, bf16[224,1024]{1,0:T(8,128)(2,1)S(1)}, u32[]{:S(2)}, u32[]{:S(2)}) %collective-permute-start.21) | collective-permute-done | bytes 458784 | tf_op jit(solution)/shard_map/ppermute | solution.py:24
  78.9 3.5 %last.1 = (f32[400,1024]{1,0:T(8,128)}, bf16[400,1024]{1,0:T(8,128)(2,1)}) custom-call(s32[400,1]{1,0:T(8,128)S(1)} %fusion.24.source_ref, bf16[224,1024]{1,0:T(8,128)(2,1)S(1)} %pad_maximum_fusion.1.mine_ref, bf16[224,1024]{1,0:T(8,128)(2,1)S(1)} %collective-permute-done.21.other_ref, bf16[1024,1024]{1,0:T(8,128)(2,1)S(1)} %get-tuple-element.16.standard_ref), custom_call_target="tpu_custom_call" | custom-call | tf_op jit(solution)/shard_map/last/pallas_call | solution.py:337
  (7 shorter events, 0.1 us)
Async XLA Ops:
  0.6 3.8 %copy-start = (s32[1024]{0:T(1024)S(1)}, s32[1024]{0:T(1024)}, u32[]{:S(2)}) copy-start(s32[1024]{0:T(1024)} %param.3) | copy-start | bytes 12292
  3.9 2.7 %collective-permute-start = (f32[224,1024]{1,0:T(8,128)S(1)}, f32[224,1024]{1,0:T(8,128)S(1)}, u32[]{:S(2)}, u32[]{:S(2)}) collective-permute-start(f32[224,1024]{1,0:T(8,128)S(1)} %get-tuple-element.17), channel_id=1, source_target_pairs={{0,1},{1,0},{2,3},{3,2},{4,5},{5,4},{6,7},{7,6},{8,9},{9,8},{10,11... | collective-permute-start | bytes 2752520 | tf_op jit(solution)/shard_map/ppermute | solution.py:24
  7.0 6.9 %collective-permute-start.1 = (s16[64,1024]{1,0:T(8,128)(2,1)S(1)}, s16[64,1024]{1,0:T(8,128)(2,1)S(1)}, u32[]{:S(2)}, u32[]{:S(2)}) collective-permute-start(s16[64,1024]{1,0:T(8,128)(2,1)S(1)} %get-tuple-element.21), channel_id=1, source_target_pairs={{0,2},{1,3},{2,0},{3,1},{4,6},{5,7},{6,4},{7,5},{8,10},{9,11},{10,... | collective-permute-start | bytes 393224 | tf_op jit(solution)/shard_map/ppermute | solution.py:24
  9.9 8.1 %collective-permute-start.2 = (s16[64,1024]{1,0:T(8,128)(2,1)S(1)}, s16[64,1024]{1,0:T(8,128)(2,1)S(1)}, u32[]{:S(2)}, u32[]{:S(2)}) collective-permute-start(s16[64,1024]{1,0:T(8,128)(2,1)S(1)} %get-tuple-element.22), channel_id=1, source_target_pairs={{0,4},{1,5},{2,6},{3,7},{4,0},{5,1},{6,2},{7,3},{8,12},{9,13},{10,... | collective-permute-start | bytes 393224 | tf_op jit(solution)/shard_map/ppermute | solution.py:24
  11.5 6.5 %collective-permute-start.3 = (s16[64,1024]{1,0:T(8,128)(2,1)S(1)}, s16[64,1024]{1,0:T(8,128)(2,1)S(1)}, u32[]{:S(2)}, u32[]{:S(2)}) collective-permute-start(s16[64,1024]{1,0:T(8,128)(2,1)S(1)} %get-tuple-element.23), channel_id=1, source_target_pairs={{0,6},{1,7},{2,4},{3,5},{4,2},{5,3},{6,0},{7,1},{8,14},{9,15},{10,... | collective-permute-start | bytes 393224 | tf_op jit(solution)/shard_map/ppermute | solution.py:24
  18.6 8.2 %collective-permute-start.6 = (s16[64,1024]{1,0:T(8,128)(2,1)S(1)}, s16[64,1024]{1,0:T(8,128)(2,1)S(1)}, u32[]{:S(2)}, u32[]{:S(2)}) collective-permute-start(s16[64,1024]{1,0:T(8,128)(2,1)S(1)} %get-tuple-element.25), channel_id=1, source_target_pairs={{0,24},{1,25},{2,26},{3,27},{4,28},{5,29},{6,30},{7,31},{8,16},{9,... | collective-permute-start | bytes 393224 | tf_op jit(solution)/shard_map/ppermute | solution.py:24
  22.3 10.2 %collective-permute-start.5 = (s16[64,1024]{1,0:T(8,128)(2,1)S(1)}, s16[64,1024]{1,0:T(8,128)(2,1)S(1)}, u32[]{:S(2)}, u32[]{:S(2)}) collective-permute-start(s16[64,1024]{1,0:T(8,128)(2,1)S(1)} %get-tuple-element.25), channel_id=1, source_target_pairs={{0,16},{1,17},{2,18},{3,19},{4,20},{5,21},{6,22},{7,23},{8,24},{9,... | collective-permute-start | bytes 393224 | tf_op jit(solution)/shard_map/ppermute | solution.py:24
  22.3 10.2 %collective-permute-start.4 = (s16[64,1024]{1,0:T(8,128)(2,1)S(1)}, s16[64,1024]{1,0:T(8,128)(2,1)S(1)}, u32[]{:S(2)}, u32[]{:S(2)}) collective-permute-start(s16[64,1024]{1,0:T(8,128)(2,1)S(1)} %get-tuple-element.25), channel_id=1, source_target_pairs={{0,8},{1,9},{2,10},{3,11},{4,12},{5,13},{6,14},{7,15},{8,0},{9,1},... | collective-permute-start | bytes 393224 | tf_op jit(solution)/shard_map/ppermute | solution.py:24
  32.9 6.9 %collective-permute-start.9 = (bf16[56,1024]{1,0:T(8,128)(2,1)S(1)}, bf16[56,1024]{1,0:T(8,128)(2,1)S(1)}, u32[]{:S(2)}, u32[]{:S(2)}) collective-permute-start(bf16[56,1024]{1,0:T(8,128)(2,1)S(1)} %shard_map.43), channel_id=1, source_target_pairs={{0,6},{1,7},{2,4},{3,5},{4,2},{5,3},{6,0},{7,1},{8,14},{9,15},{10,... | collective-permute-start | bytes 344072 | tf_op jit(solution)/shard_map/ppermute | solution.py:24
  34.5 6.0 %collective-permute-start.8 = (bf16[56,1024]{1,0:T(8,128)(2,1)S(1)}, bf16[56,1024]{1,0:T(8,128)(2,1)S(1)}, u32[]{:S(2)}, u32[]{:S(2)}) collective-permute-start(bf16[56,1024]{1,0:T(8,128)(2,1)S(1)} %shard_map.43), channel_id=1, source_target_pairs={{0,4},{1,5},{2,6},{3,7},{4,0},{5,1},{6,2},{7,3},{8,12},{9,13},{10,... | collective-permute-start | bytes 344072 | tf_op jit(solution)/shard_map/ppermute | solution.py:24
  36.0 4.9 %collective-permute-start.7 = (bf16[56,1024]{1,0:T(8,128)(2,1)S(1)}, bf16[56,1024]{1,0:T(8,128)(2,1)S(1)}, u32[]{:S(2)}, u32[]{:S(2)}) collective-permute-start(bf16[56,1024]{1,0:T(8,128)(2,1)S(1)} %shard_map.43), channel_id=1, source_target_pairs={{0,2},{1,3},{2,0},{3,1},{4,6},{5,7},{6,4},{7,5},{8,10},{9,11},{10,... | collective-permute-start | bytes 344072 | tf_op jit(solution)/shard_map/ppermute | solution.py:24
  40.9 1.9 %collective-permute-start.10 = (bf16[224,1024]{1,0:T(8,128)(2,1)S(1)}, bf16[224,1024]{1,0:T(8,128)(2,1)S(1)}, u32[]{:S(2)}, u32[]{:S(2)}) collective-permute-start(bf16[224,1024]{1,0:T(8,128)(2,1)S(1)} %pad_maximum_fusion), channel_id=1, source_target_pairs={{0,1},{1,0},{2,3},{3,2},{4,5},{5,4},{6,7},{7,6},{8,9},{9,8},{10,11... | collective-permute-start | bytes 1376264 | tf_op jit(solution)/shard_map/ppermute | solution.py:24
  44.4 2.5 %collective-permute-start.11 = (f32[224,1024]{1,0:T(8,128)S(1)}, f32[224,1024]{1,0:T(8,128)S(1)}, u32[]{:S(2)}, u32[]{:S(2)}) collective-permute-start(f32[224,1024]{1,0:T(8,128)S(1)} %fusion.7), channel_id=1, source_target_pairs={{0,1},{1,0},{2,3},{3,2},{4,5},{5,4},{6,7},{7,6},{8,9},{9,8},{10,11... | collective-permute-start | bytes 2752520 | tf_op jit(solution)/shard_map/ppermute | solution.py:24
  47.1 6.1 %collective-permute-start.12 = (f16[56,1024]{1,0:T(8,128)(2,1)S(1)}, f16[56,1024]{1,0:T(8,128)(2,1)S(1)}, u32[]{:S(2)}, u32[]{:S(2)}) collective-permute-start(f16[56,1024]{1,0:T(8,128)(2,1)S(1)} %get-tuple-element.30), channel_id=1, source_target_pairs={{0,2},{1,3},{2,0},{3,1},{4,6},{5,7},{6,4},{7,5},{8,10},{9,11},{10,... | collective-permute-start | bytes 344072 | tf_op jit(solution)/shard_map/ppermute | solution.py:24
  48.4 7.2 %collective-permute-start.14 = (f16[56,1024]{1,0:T(8,128)(2,1)S(1)}, f16[56,1024]{1,0:T(8,128)(2,1)S(1)}, u32[]{:S(2)}, u32[]{:S(2)}) collective-permute-start(f16[56,1024]{1,0:T(8,128)(2,1)S(1)} %get-tuple-element.31), channel_id=1, source_target_pairs={{0,6},{1,7},{2,4},{3,5},{4,2},{5,3},{6,0},{7,1},{8,14},{9,15},{10,... | collective-permute-start | bytes 344072 | tf_op jit(solution)/shard_map/ppermute | solution.py:24
  49.9 7.1 %collective-permute-start.13 = (f16[56,1024]{1,0:T(8,128)(2,1)S(1)}, f16[56,1024]{1,0:T(8,128)(2,1)S(1)}, u32[]{:S(2)}, u32[]{:S(2)}) collective-permute-start(f16[56,1024]{1,0:T(8,128)(2,1)S(1)} %get-tuple-element.32), channel_id=1, source_target_pairs={{0,4},{1,5},{2,6},{3,7},{4,0},{5,1},{6,2},{7,3},{8,12},{9,13},{10,... | collective-permute-start | bytes 344072 | tf_op jit(solution)/shard_map/ppermute | solution.py:24
  57.1 7.9 %collective-permute-start.17 = (f16[56,1024]{1,0:T(8,128)(2,1)S(1)}, f16[56,1024]{1,0:T(8,128)(2,1)S(1)}, u32[]{:S(2)}, u32[]{:S(2)}) collective-permute-start(f16[56,1024]{1,0:T(8,128)(2,1)S(1)} %fusion.19), channel_id=1, source_target_pairs={{0,24},{1,25},{2,26},{3,27},{4,28},{5,29},{6,30},{7,31},{8,16},{9,... | collective-permute-start | bytes 344072 | tf_op jit(solution)/shard_map/ppermute | solution.py:24
  58.9 9.3 %collective-permute-start.16 = (f16[56,1024]{1,0:T(8,128)(2,1)S(1)}, f16[56,1024]{1,0:T(8,128)(2,1)S(1)}, u32[]{:S(2)}, u32[]{:S(2)}) collective-permute-start(f16[56,1024]{1,0:T(8,128)(2,1)S(1)} %fusion.19), channel_id=1, source_target_pairs={{0,16},{1,17},{2,18},{3,19},{4,20},{5,21},{6,22},{7,23},{8,24},{9,... | collective-permute-start | bytes 344072 | tf_op jit(solution)/shard_map/ppermute | solution.py:24
  59.0 9.3 %collective-permute-start.15 = (f16[56,1024]{1,0:T(8,128)(2,1)S(1)}, f16[56,1024]{1,0:T(8,128)(2,1)S(1)}, u32[]{:S(2)}, u32[]{:S(2)}) collective-permute-start(f16[56,1024]{1,0:T(8,128)(2,1)S(1)} %fusion.19), channel_id=1, source_target_pairs={{0,8},{1,9},{2,10},{3,11},{4,12},{5,13},{6,14},{7,15},{8,0},{9,1},... | collective-permute-start | bytes 344072 | tf_op jit(solution)/shard_map/ppermute | solution.py:24
  68.5 7.0 %collective-permute-start.20 = (bf16[56,1024]{1,0:T(8,128)(2,1)S(1)}, bf16[56,1024]{1,0:T(8,128)(2,1)S(1)}, u32[]{:S(2)}, u32[]{:S(2)}) collective-permute-start(bf16[56,1024]{1,0:T(8,128)(2,1)S(1)} %multiply_convert_fusion), channel_id=1, source_target_pairs={{0,6},{1,7},{2,4},{3,5},{4,2},{5,3},{6,0},{7,1},{8,14},{9,15},{10,... | collective-permute-start | bytes 344072 | tf_op jit(solution)/shard_map/ppermute | solution.py:24
  70.0 7.0 %collective-permute-start.19 = (bf16[56,1024]{1,0:T(8,128)(2,1)S(1)}, bf16[56,1024]{1,0:T(8,128)(2,1)S(1)}, u32[]{:S(2)}, u32[]{:S(2)}) collective-permute-start(bf16[56,1024]{1,0:T(8,128)(2,1)S(1)} %multiply_convert_fusion), channel_id=1, source_target_pairs={{0,4},{1,5},{2,6},{3,7},{4,0},{5,1},{6,2},{7,3},{8,12},{9,13},{10,... | collective-permute-start | bytes 344072 | tf_op jit(solution)/shard_map/ppermute | solution.py:24
  71.1 5.9 %collective-permute-start.18 = (bf16[56,1024]{1,0:T(8,128)(2,1)S(1)}, bf16[56,1024]{1,0:T(8,128)(2,1)S(1)}, u32[]{:S(2)}, u32[]{:S(2)}) collective-permute-start(bf16[56,1024]{1,0:T(8,128)(2,1)S(1)} %multiply_convert_fusion), channel_id=1, source_target_pairs={{0,2},{1,3},{2,0},{3,1},{4,6},{5,7},{6,4},{7,5},{8,10},{9,11},{10,... | collective-permute-start | bytes 344072 | tf_op jit(solution)/shard_map/ppermute | solution.py:24
  77.0 1.9 %collective-permute-start.21 = (bf16[224,1024]{1,0:T(8,128)(2,1)S(1)}, bf16[224,1024]{1,0:T(8,128)(2,1)S(1)}, u32[]{:S(2)}, u32[]{:S(2)}) collective-permute-start(bf16[224,1024]{1,0:T(8,128)(2,1)S(1)} %pad_maximum_fusion.1.mine_ref), channel_id=1, source_target_pairs={{0,1},{1,0},{2,3},{3,2},{4,5},{5,4},{6,7},{7,6},{8,9},{9,8},{10,11... | collective-permute-start | bytes 1376264 | tf_op jit(solution)/shard_map/ppermute | solution.py:24
